TPU v7x, 32 devices: a whole 2x2x4 slice. The times are simulated.
32 devices in a mesh: parts: 2 (over y), gx: 4 (over z), gy: 2 (over x), gz: 2 (over core).
Axes of the slice: x: 2, y: 2, z: 4, core: 2. Of those that a mesh axis runs over, the one named last changes fastest.
Arguments:
- volume: bfloat16 [56, 14, 56, 48], P(('parts', 'gx'), 'gy', 'gz'), parts along dimension 0, may hold values from -6 to 6
- w_qkv: bfloat16 [2, 48, 144], replicated, may hold values from -3 to 3
- w_proj: bfloat16 [2, 48, 48], replicated, may hold values from -0.875 to 0.875
- w_up: bfloat16 [2, 48, 192], replicated, may hold values from -0.875 to 0.875
- w_down: bfloat16 [2, 192, 48], replicated, may hold values from -0.4375 to 0.4375
- norm_gain: float32 [2, 2, 48], replicated, may hold values from 0.25 to 1.75
- conv_weight: bfloat16 [27, 48, 48], replicated, may hold values from -0.15625 to 0.15625
- conv_gain: float32 [48], replicated, may hold values from 0.25 to 1.75
Outputs:
- features: bfloat16 [56, 14, 56, 48], P(('parts', 'gx'), 'gy', 'gz'), parts along dimension 0
There are 2 independent parts, one for each index of `parts`. A program takes and returns all parts, laid end to end along the dimension named above; an argument that names none is the same for every part. Nothing has to cross between parts.
All inputs are finite; a program needn't handle non-finite values.
Results may differ from a plain program's by a relative error of at most 0.039.
The roundings to bfloat16 on the way count: a program that leaves them out, or rounds other values in their place, can miss the bound.
Values may be sent and summed in bfloat16 or wider, within the bound.
No kernel may reach another device: no remote copies, remote signals or barrier semaphores. Data moves between devices by JAX's collectives and lax.ppermute only.
A program may use at most 64 MiB of HBM per device.

v0:
```python
import functools

import jax
import jax.numpy as jnp
import numpy as np
from jax import lax
from jax.experimental import pallas as pl
from jax.experimental.pallas import tpu as pltpu
from jax.sharding import PartitionSpec as P


HEADS = 3
WINDOW = 7
SHIFT = 3
LANES = 128
HALF = 64
ROWS = 8
BIG = -1e30
HIGH = WINDOW - SHIFT
EXT = 2 * WINDOW + 1
BF = jnp.bfloat16
F32 = jnp.float32


def mm(a, b):
    return jnp.dot(a, b, preferred_element_type=F32)


def iota(shape, dim):
    return lax.broadcasted_iota(jnp.int32, shape, dim)


def norm_cols(x, gain, width):
    mean = jnp.sum(x, 0, keepdims=True) * (1.0 / width)
    centred = x - mean
    spread = jnp.sum(centred * centred, 0, keepdims=True) * (1.0 / width)
    return centred * lax.rsqrt(spread + 1e-05) * gain


def twice_gelu(x):
    inner = x * (0.7978845608028654 + (0.7978845608028654 * 0.044715) * (x * x))
    return x + x * jnp.tanh(inner)


def block_weights(b, wqkv_ref, wproj_ref, wup_ref, wdown_ref, gain_ref):
    wqkv = wqkv_ref[b]
    width, triple = wqkv.shape
    scale = (width // HEADS) ** (-0.5)
    i, j = iota((triple, LANES), 0), iota((triple, LANES), 1)
    take_v = (j < width) & (i == j + 2 * width)
    take_q = (j >= HALF) & (j < HALF + width) & (i == j - HALF)
    place = jnp.where(take_v, 1.0, jnp.where(take_q, scale, 0.0)).astype(BF)
    wvq = mm(wqkv, place).astype(BF)
    o, i = iota((width, triple), 0), iota((width, triple), 1)
    place = jnp.where(i == o + width, 1.0, 0.0).astype(BF)
    wk = lax.dot_general(place, wqkv, (((1,), (1,)), ((), ())), preferred_element_type=F32).astype(BF)
    gains = gain_ref[b]
    diagonal = iota((width, width), 0) == iota((width, width), 1)
    first, second = [jnp.sum(jnp.where(diagonal, gains[k : k + 1], 0.0), 1, keepdims=True) for k in range(2)]
    i, j = iota((width, LANES), 0), iota((width, LANES), 1)
    spread = jnp.where(i == j, 1.0, 0.0).astype(BF)
    wp = lax.dot_general(wproj_ref[b], spread, (((0,), (0,)), ((), ())), preferred_element_type=F32)
    wp = (wp + jnp.where(j == i + HALF, 1.0, 0.0)).astype(BF)
    return wvq, wk, first, wp, wup_ref[b], wdown_ref[b] * jnp.asarray(0.5, BF), second


def make_keys(columns, bias, wts, width):
    wvq, wk, gain = wts[0], wts[1], wts[2]
    normed = norm_cols(columns, gain, width).astype(BF)
    vq = lax.dot_general(normed, wvq, (((0,), (0,)), ((), ())), preferred_element_type=F32)
    kt = mm(wk, normed).astype(BF)
    keys = columns.shape[1]
    top = iota((HALF - width, keys), 0) == 0
    extra = jnp.where(top, bias, 0.0).astype(BF)
    kaug = jnp.concatenate([jnp.zeros((HALF, keys), BF), kt, extra], 0)
    return vq, kaug


def values_of(vq, width):
    return jnp.where(iota(vq.shape, 1) < width, vq, 1.0).astype(BF)


def queries_of(rows, width):
    head_dim = width // HEADS
    lane = iota(rows.shape, 1)
    one = jnp.where(lane == HALF + width, 1.0, 0.0)
    parts = []
    for h in range(HEADS):
        low = HALF + h * head_dim
        parts.append(jnp.where((lane >= low) & (lane < low + head_dim), rows, one))
    spare = -len(parts) * rows.shape[0] % 32
    if spare:
        parts.append(jnp.zeros((spare, LANES), F32))
    return jnp.concatenate(parts, 0).astype(BF)


def attend(jobs, width, between=None):
    head_dim = width // HEADS
    jobs = list(jobs)
    ahead = mm(jobs[0][0][...], jobs[0][1][...])
    for i, (_, _, values, n, store) in enumerate(jobs):
        scores = ahead
        if i + 1 < len(jobs):
            ahead = mm(jobs[i + 1][0][...], jobs[i + 1][1][...])
        if between is not None:
            between(i)
        top = jnp.max(scores, -1, keepdims=True)
        weights = jnp.exp(scores - top).astype(BF)
        out = mm(weights, values[...])
        lane = iota((n, LANES), 1)
        lane = jnp.where(lane >= HALF, lane - HALF, lane)
        mixed = out[:n]
        for h in range(1, HEADS):
            mixed = jnp.where(lane >= h * head_dim, out[h * n : (h + 1) * n], mixed)
        store(mixed / pltpu.roll(mixed, HALF, 1))


def feed(first, wts, width):
    wup, wdown, gain = wts[4:]
    first = first.astype(BF).astype(F32)
    normed = norm_cols(first, gain, width).astype(BF)
    upper = lax.dot_general(wup, normed, (((0,), (0,)), ((), ())), preferred_element_type=F32)
    return (first + mm(wdown, twice_gelu(upper).astype(BF))).astype(BF).astype(F32)


def against_rows(w, rows):
    return lax.dot_general(w, rows, (((1,), (1,)), ((), ())), preferred_element_type=F32)


def first_kernel(width, ny, *refs):
    hbm, out_ref = refs[:7], refs[7]
    y_refs, x_refs = refs[8 : 8 + ny], refs[8 + ny : 10 + ny]
    copies = refs[10 + ny : 17 + ny]
    sems = refs[17 + ny]
    raw, tok, qs, ks, vs, mix, held, done = refs[18 + ny :]
    moves = [pltpu.make_async_copy(h, v, sems.at[i]) for i, (h, v) in enumerate(zip(hbm, copies))]
    for m in moves:
        m.start()
    for m in moves[1:]:
        m.wait()
    vol_ref, geo_ref, wqkv_ref, wproj_ref, wup_ref, wdown_ref, gain_ref = copies
    nz = vol_ref.shape[2]
    groups = nz // WINDOW
    spots = WINDOW * WINDOW
    kept = spots - 1
    keys = kept * ROWS
    wts = block_weights(0, wqkv_ref, wproj_ref, wup_ref, wdown_ref, gain_ref)
    done[...] = jnp.zeros(done.shape, F32)
    moves[0].wait()
    raw[:, nz:, :] = jnp.zeros((spots, raw.shape[1] - nz, LANES), F32)
    raw[:, 0:nz, 0:width] = vol_ref[...].astype(F32).reshape(spots, nz, width)
    bias = jnp.where(geo_ref[8:9, :] < WINDOW, 0.0, BIG)

    def make(w):
        tok[w] = raw[0:kept, WINDOW * w : WINDOW * w + ROWS, :]
        for j in range(WINDOW):
            tok[w, j, WINDOW : WINDOW + 1, :] = raw[kept, WINDOW * w + j : WINDOW * w + j + 1, :]
        columns = jnp.transpose(tok[w].reshape(keys, LANES))[:width]
        held[:, keys * w : keys * (w + 1)] = columns
        vq, kaug = make_keys(columns, bias, wts, width)
        vs[w] = values_of(vq, width)
        ks[w] = kaug
        qs[w] = queries_of(vq, width)

    def finish(w0, n):
        mixed = mix[w0 : w0 + n].reshape(n * keys, LANES)[:, :width].astype(BF)
        first = held[:, keys * w0 : keys * (w0 + n)] + against_rows(wts[3][:, :width], mixed)
        out = feed(first, wts, width)
        out = jnp.transpose(jnp.concatenate([out, jnp.zeros((LANES - width, n * keys), F32)], 0))[:, :width]
        out = out.reshape(n, kept, ROWS, width)
        for w in range(w0, w0 + n):
            done[0:kept, WINDOW * w : WINDOW * (w + 1), :width] = out[w - w0, :, :WINDOW, :]
            if w == 0:
                done[0:kept, nz : nz + SHIFT, :width] = out[w - w0, :, :SHIFT, :]
            for j in range(WINDOW):
                one = out[w - w0, j, WINDOW : WINDOW + 1, :]
                done[kept, WINDOW * w + j : WINDOW * w + j + 1, :width] = one
                if w == 0 and j < SHIFT:
                    done[kept, nz + j : nz + j + 1, :width] = one

    for w in range(groups):
        make(w)

    def keep(w):
        def store(v):
            mix[w] = v

        return store

    attend([(qs.at[w], ks.at[w], vs.at[w], keys, keep(w)) for w in range(groups)], width)
    finish(0, groups)
    pieces = [done[:, SHIFT + WINDOW * w : SHIFT + WINDOW * w + ROWS, :] for w in range(groups)]
    rolled = [pltpu.roll(p.reshape(spots * ROWS, LANES), HALF, 1).reshape(spots, ROWS, LANES) for p in pieces[1::2]]
    joined = [a + b for a, b in zip(pieces[0::2], rolled)]
    packed = jnp.concatenate(joined, 1).astype(BF)
    out_ref[...] = packed.reshape(WINDOW, WINDOW, ROWS * len(joined), LANES)
    yodd = lax.axis_index("gy") % 2
    for k, y_ref in enumerate(y_refs):
        start = jnp.where((yodd + k) % 2 == 0, SHIFT, 0)
        y_ref[...] = out_ref[:, pl.ds(start, HIGH)]
    xodd = lax.axis_index("gx") % 2
    for k, x_ref in enumerate(x_refs):
        start = jnp.where((xodd + k) % 2 == 0, SHIFT, 0)
        x_ref[...] = out_ref[pl.ds(start, HIGH)]


BOXES = ((SHIFT, HIGH), (0, HIGH + 1))
COLUMNS = tuple((wx, wy) for wx in range(2) for wy in range(2))


def box_rows(wx, wy):
    return BOXES[wx][1] * BOXES[wy][1] * ROWS


def layout(cols):
    sizes = [box_rows(*COLUMNS[c]) for c in cols]
    return {c: sum(sizes[:i]) for i, c in enumerate(cols)}, sum(sizes)


def half_columns(wy):
    return [c for c, column in enumerate(COLUMNS) if column[1] == wy]


def up(n, m):
    return -(-n // m) * m


def feed_rows(mix, stop, wts, width):
    out = feed(against_rows(wts[3], mix[:stop].astype(BF)), wts, width)
    nil = jnp.zeros((HALF - width, stop), F32)
    return jnp.transpose(jnp.concatenate([out, nil, out, nil], 0))


def position():
    index = [lax.axis_index(a) for a in ("gx", "gy", "gz")]
    count = [lax.axis_size(a) for a in ("gx", "gy", "gz")]
    return index, count


def place_all(ext, split, pieces, shared):
    for tile, other, x, y in pieces:
        nx, ny = tile.shape[:2]
        n = nx * ny
        tile = tile.astype(F32).reshape(n, tile.shape[2], LANES)
        if other is not None:
            other = other.astype(F32).reshape(n, ROWS, LANES)
        for slab, v in enumerate(split(tile, other)):
            ext[slab, pl.ds(x, nx), pl.ds(y, ny)] = v.reshape(nx, ny, ROWS, LANES)
    for wx, wy in shared:
        x0, y0 = WINDOW * wx, WINDOW * wy
        gone = (WINDOW * WINDOW - 1) * wx
        for slab in range(ext.shape[0]):
            for j in range(WINDOW):
                to = j + 1 - wx
                ext[slab, x0 + to // WINDOW, y0 + to % WINDOW, WINDOW : WINDOW + 1, :] = ext[
                    slab, x0 + gone // WINDOW, y0 + gone % WINDOW, j : j + 1, :
                ]


def window_attention(width, groups, cols, work, start_of, geo_ref, wts, ext, mix, ks, vs, qs, between=None):
    index, count = position()
    spots = WINDOW * WINDOW
    keys = (spots - 1) * ROWS
    nolow = [jnp.where(i > 0, 0.0, 1.0) for i in index]
    nohigh = [jnp.where(i < c - 1, 0.0, 1.0) for i, c in zip(index, count)]

    def turn(slab, c):
        wx, wy = COLUMNS[c]
        first = ROWS * (1 - wx)
        tokens = ext[slab, WINDOW * wx : WINDOW * (wx + 1), WINDOW * wy : WINDOW * (wy + 1)]
        flat = tokens.reshape(spots * ROWS, LANES)
        return tokens, jnp.transpose(flat[first : first + keys])

    def make(slab, c, tokens, turned):
        wx, wy = COLUMNS[c]
        row, px, py = [geo_ref[8 * wx + k : 8 * wx + k + 1, :] for k in range(3)]
        badx = jnp.where(px < HIGH, nolow[0], 0.0) if wx == 0 else jnp.where(px >= HIGH, nohigh[0], 0.0)
        bady = jnp.where(py < HIGH, nolow[1], 0.0) if wy == 0 else jnp.where(py >= HIGH, nohigh[1], 0.0)
        bad = badx + bady + jnp.where(row < WINDOW, 0.0, 1.0)
        (bx, nx), (by, ny) = BOXES[wx], BOXES[wy]
        nq = nx * ny * ROWS
        first = ROWS * (1 - wx)
        chosen = tokens[bx : bx + nx, by : by + ny].reshape(nq, LANES)
        for slot, (at, half, g) in enumerate(work):
            if at != slab:
                continue
            badz = jnp.zeros_like(bad)
            if g == 0:
                badz = jnp.where(row < HIGH, nolow[2], 0.0)
            if g == groups - 1:
                badz = jnp.where(row >= HIGH, nohigh[2], 0.0)
            bias = jnp.where(bad + badz > 0.0, BIG, 0.0)
            vq, kaug = make_keys(turned[HALF * half : HALF * half + width], bias, wts, width)
            vs[c, slot] = values_of(vq, width)
            ks[c, slot] = kaug
            picked = [
                vq[ROWS * (WINDOW * x + by) - first : ROWS * (WINDOW * x + by + ny) - first] for x in range(bx, bx + nx)
            ]
            qs[c][slot] = queries_of(jnp.concatenate(picked, 0), width)
            start = start_of(g, c)
            mix[start : start + nq, HALF:] = (chosen if half else pltpu.roll(chosen, HALF, 1))[:, HALF:]

    order = [(slab, c) for slab in sorted({w[0] for w in work}) for c in cols]
    ahead = turn(*order[0])
    for i, at in enumerate(order):
        now = ahead
        if i + 1 < len(order):
            ahead = turn(*order[i + 1])
        make(*at, *now)

    def job(slot, c):
        n = box_rows(*COLUMNS[c])
        start = start_of(work[slot][2], c)

        def store(v):
            mix[start : start + n, :HALF] = v[:, :HALF]

        return qs[c].at[slot], ks.at[c, slot], vs.at[c, slot], n, store

    attend([job(slot, c) for slot in range(len(work)) for c in cols], width, between)


def inner_kernel(width, ypieces, part, geo_ref, *refs):
    pieces = refs[:3] if part < 0 else refs[: 3 * (ypieces + 1)]
    rest = refs[len(pieces) :]
    wqkv_ref, wproj_ref, wup_ref, wdown_ref, gain_ref, out_ref, mix, ext, ks, vs = rest[:10]
    qs = rest[10:]
    pairs = pieces[0].shape[2] // ROWS
    work = [(p, half, 1 + 2 * p + half) for p in range(pairs) for half in range(2)][:-1]
    index, _ = position()
    far = WINDOW + HIGH
    xa, xb = [jnp.where(index[0] % 2 == k, far, 0) for k in (0, 1)]
    ys = [jnp.where(index[1] % 2 == k, far, 0) for k in range(2)]
    wts = block_weights(1, wqkv_ref, wproj_ref, wup_ref, wdown_ref, gain_ref)
    tiles = []
    for k, y in enumerate([HIGH] + ys[: len(pieces) // 3 - 1]):
        for i, x in enumerate((HIGH, xa, xb)):
            tiles.append((pieces[3 * k + i][...], None, x, y))
    if part < 0:
        ext[:, :, pl.ds(ys[1], HIGH)] = jnp.zeros((pairs, EXT, HIGH, ROWS, LANES), F32)

    def split(tile, other):
        return [tile[:, p * ROWS : (p + 1) * ROWS, :] for p in range(pairs)]

    def run(cols):
        places, rows = layout(cols)
        used = rows * len(work)
        rows_ref = mix if part < 0 else out_ref
        rest = rows_ref.shape[0] - used
        if rest:
            rows_ref[used:] = jnp.zeros((rest, LANES), F32)
        place_all(ext, split, tiles, [COLUMNS[c] for c in cols])
        start = lambda g, c: rows * (g - 1) + places[c]
        window_attention(width, 2 * pairs + 1, cols, work, start, geo_ref, wts, ext, rows_ref, ks, vs, qs)
        if part < 0:
            stop = up(used, LANES)
            out_ref[:stop] = feed_rows(mix, stop, wts, width)
            if stop < out_ref.shape[0]:
                out_ref[stop:] = jnp.zeros((out_ref.shape[0] - stop, LANES), F32)

    if part == 0:
        run(list(range(len(COLUMNS))))
    else:
        for side in range(2):

            @pl.when(index[1] % 2 == side)
            def _(side=side):
                run(half_columns(side if part < 0 else 1 - side))


def last_kernel(width, ypieces, geo_ref, inner_ref, *refs):
    early = ypieces == 1
    if early:
        free_ref, *refs = refs
    pieces = refs[: 4 * (ypieces + 1)]
    rest = refs[4 * (ypieces + 1) :]
    wqkv_ref, wproj_ref, wup_ref, wdown_ref, gain_ref, wconv_hbm, cgain_hbm, out_ref = rest[:8]
    ext, mix, fed, grid, wc, tot, wconv_ref, cgain_ref, sems, ks, vs = rest[8:19]
    qs = rest[19:]
    moves = [
        pltpu.make_async_copy(wconv_hbm, wconv_ref, sems.at[0]),
        pltpu.make_async_copy(cgain_hbm, cgain_ref, sems.at[1]),
    ]
    for m in moves:
        m.start()
    nz = out_ref.shape[2]
    pairs = pieces[0].shape[2] // ROWS
    groups = 2 * pairs + 1
    index, count = position()
    far = WINDOW + HIGH
    xa, xb = [jnp.where(index[0] % 2 == k, far, 0) for k in (0, 1)]
    ys = [jnp.where(index[1] % 2 == k, far, 0) for k in range(2)]
    wts = block_weights(1, wqkv_ref, wproj_ref, wup_ref, wdown_ref, gain_ref)
    tiles = []
    for k, y in enumerate([HIGH] + ys[:ypieces]):
        at = 0
        for i, x in enumerate((HIGH, xa, xb)):
            mine = pieces[4 * k + i][:, :, -ROWS:, :]
            tiles.append((mine, pieces[4 * k + 3][at : at + mine.shape[0]], x, y))
            at += mine.shape[0]
    if ypieces == 1:
        ext[:, :, pl.ds(ys[1], HIGH)] = jnp.zeros((2, EXT, HIGH, ROWS, LANES), F32)

    def split(mine, other):
        low = iota(mine.shape, 1) < HIGH
        return jnp.where(low, mine, other), jnp.where(low, other, mine)

    cols = list(range(len(COLUMNS)))
    offsets, per = layout(cols)
    depth = grid.shape[2]
    grid[:, :, WINDOW * groups :] = jnp.zeros((WINDOW + 2, WINDOW + 2, depth - WINDOW * groups, LANES), F32)

    def scatter(g, rows, base, cols):
        places, _ = layout(cols)
        for c in cols:
            wx, wy = COLUMNS[c]
            (_, nx), (_, ny) = BOXES[wx], BOXES[wy]
            for x in range(nx):
                for y in range(ny):
                    at = base + places[c] + ROWS * (x * ny + y)
                    grid[HIGH * wx + x, HIGH * wy + y, WINDOW * g : WINDOW * (g + 1), :] = rows[at : at + WINDOW]

    used = 2 * per
    stop = up(used, LANES)
    mix[used:stop] = jnp.zeros((stop - used, LANES), F32)
    fed[...] = feed_rows(inner_ref, inner_ref.shape[0], wts, width)
    place_all(ext, split, tiles, COLUMNS)
    work = [(0, 1, groups - 1), (1, 1, 0)]
    start = lambda g, c: (per if g else 0) + offsets[c]
    window_attention(width, groups, cols, work, start, geo_ref, wts, ext, mix, ks, vs, qs)
    out = feed_rows(mix, stop, wts, width)
    scatter(0, out, 0, cols)
    scatter(groups - 1, out, per, cols)
    if early:
        for side in range(2):

            @pl.when(index[1] % 2 == side)
            def _(side=side):
                for wy, rows in ((side, free_ref), (1 - side, fed)):
                    half = half_columns(wy)
                    for g in range(1, groups - 1):
                        scatter(g, rows, layout(half)[1] * (g - 1), half)

    else:
        for g in range(1, groups - 1):
            scatter(g, fed, per * (g - 1), cols)

    last = WINDOW + 1

    def clear(when, *at):
        @pl.when(when)
        def _():
            grid[at] = jnp.zeros_like(grid[at])

    clear(index[0] == 0, slice(0, 1))
    clear(index[0] == count[0] - 1, slice(last, last + 1))
    clear(index[1] == 0, slice(None), slice(0, 1))
    clear(index[1] == count[1] - 1, slice(None), slice(last, last + 1))
    clear(index[2] == 0, slice(None), slice(None), slice(SHIFT, HIGH))
    clear(index[2] == count[2] - 1, slice(None), slice(None), slice(HIGH + nz, HIGH + nz + 1))

    for m in moves:
        m.wait()
    wc[...] = jnp.zeros(wc.shape, BF)
    for dx in range(3):
        total = None
        for dy in range(3):
            taps = wconv_ref[9 * dx + 3 * dy : 9 * dx + 3 * dy + 3].reshape(3 * width, width)
            i, j = iota((width, 4 * HALF), 0), iota((width, 4 * HALF), 1)
            place = jnp.where(j == i + HALF * dy, 1.0, 0.0).astype(BF)
            part = mm(taps, place)
            total = part if total is None else total + part
        for dz in range(3):
            at = 4 * HALF * dx + HALF * dz
            wc[at : at + width] = total[width * dz : width * (dz + 1)].astype(BF)

    side = WINDOW + 2
    padded = -(-nz // 16) * 16

    def lhs(x):
        taps = [grid[x, :, SHIFT + d : SHIFT + d + padded, :].reshape(side * padded, LANES) for d in range(3)]
        lower = iota(taps[0].shape, 1) < HALF
        return jnp.concatenate([jnp.where(lower, taps[0], taps[1]), taps[2]], 1).astype(BF)

    rows = [lhs(x) for x in range(side)]
    acc = mm(jnp.concatenate([jnp.concatenate(rows[x : x + 3], 1) for x in range(WINDOW)], 0), wc[...])
    strip = WINDOW * padded
    for x in range(WINDOW):
        part = acc[x * side * padded : (x + 1) * side * padded]
        near, second = part[:, :LANES], part[:, LANES:]
        turned = pltpu.roll(near[padded : (WINDOW + 1) * padded], HALF, 1)
        tot[x * strip : (x + 1) * strip] = near[:strip] + turned + second[2 * padded :]
    tot[WINDOW * strip :] = jnp.zeros((tot.shape[0] - WINDOW * strip, LANES), F32)
    diagonal = iota((width, width), 0) == iota((width, width), 1)
    cg = jnp.sum(jnp.where(diagonal, cgain_ref[...], 0.0), 1, keepdims=True)
    normed = norm_cols(jnp.transpose(tot[...])[:width], cg, width)
    active = jnp.where(normed >= 0.0, normed, 0.01 * normed)
    active = jnp.transpose(jnp.concatenate([active, jnp.zeros((LANES - width, tot.shape[0]), F32)], 0))
    for x in range(WINDOW):
        centre = grid[x + 1, 1 : 1 + WINDOW, HIGH : HIGH + padded, :].reshape(strip, LANES)
        result = (centre + active[x * strip : (x + 1) * strip]).reshape(WINDOW, padded, LANES).astype(BF)
        out_ref[x] = result[:, :nz, :width]


def geometry():
    kept = WINDOW * WINDOW - 1
    geo = np.full((16, kept * ROWS), WINDOW, np.float32)
    for v in range(2):
        gone = kept * v
        for i in range(kept):
            spot = i + 1 - v
            for r in range(ROWS):
                t = i * ROWS + r
                if r < WINDOW:
                    geo[8 * v : 8 * v + 3, t] = r, spot // WINDOW, spot % WINDOW
                elif i < WINDOW:
                    geo[8 * v : 8 * v + 3, t] = i, gone // WINDOW, gone % WINDOW
                else:
                    geo[8 * v + 1 : 8 * v + 3, t] = spot // WINDOW, spot % WINDOW
    return jnp.asarray(geo)


def exchange(v, axis, odd):
    count, cores = lax.axis_size(axis), lax.axis_size("gz")
    pairs = []
    for i in range(count):
        low = i - (i - odd) % 2
        for c in range(cores):
            if low < 0 or low + 1 >= count:
                to = (i, c ^ 1 if c ^ 1 < cores else c)
            else:
                to = (low + 1 if i == low else low, c)
            pairs.append((i * cores + c, to[0] * cores + to[1]))
    return lax.ppermute(v, (axis, "gz"), pairs)


def body(volume, w_qkv, w_proj, w_up, w_down, norm_gain, conv_weight, conv_gain):
    sx, sy, sz, width = volume.shape
    spots = sx * sy
    groups = sz // WINDOW
    geo = geometry()
    keys = (spots - 1) * ROWS
    weights = (w_qkv, w_proj, w_up, jnp.swapaxes(w_down, 1, 2), norm_gain)
    halves = [0] if lax.axis_size("gy") == 2 else [0, 1]
    tall = ROWS * groups // 2

    operands = (volume, geo, *weights)
    packed, *cuts = pl.pallas_call(
        functools.partial(first_kernel, width, len(halves)),
        out_shape=[jax.ShapeDtypeStruct((sx, sy, tall, LANES), BF)]
        + [jax.ShapeDtypeStruct((sx, HIGH, tall, LANES), BF) for _ in halves]
        + [jax.ShapeDtypeStruct((HIGH, sy, tall, LANES), BF) for _ in range(2)],
        in_specs=[pl.BlockSpec(memory_space=pltpu.HBM)] * len(operands),
        scratch_shapes=[pltpu.VMEM(v.shape, v.dtype) for v in operands]
        + [
            pltpu.SemaphoreType.DMA((len(operands),)),
            pltpu.VMEM((spots, sz + 12, LANES), F32),
            pltpu.VMEM((groups, spots - 1, ROWS, LANES), F32),
            pltpu.VMEM((groups, HEADS * keys, LANES), BF),
            pltpu.VMEM((groups, LANES, keys), BF),
            pltpu.VMEM((groups, keys, LANES), BF),
            pltpu.VMEM((groups, keys, LANES), F32),
            pltpu.VMEM((width, groups * keys), F32),
            pltpu.VMEM((spots, sz + 12, LANES), F32),
        ],
        compiler_params=pltpu.CompilerParams(vmem_limit_bytes=24 << 20),
        name="first_block",
    )(*[pltpu.with_memory_space_constraint(v, pltpu.HBM) for v in operands])

    xodd = lax.axis_index("gx") % 2

    def cut(v, odd):
        return lax.dynamic_slice_in_dim(v, jnp.where(odd == 0, SHIFT, 0), HIGH, 0)

    def other_core(v):
        return lax.ppermute(v, "gz", [(0, 1), (1, 0)])

    ys = [exchange(v, "gy", k) for k, v in zip(halves, cuts)]
    xs = [exchange(v, "gx", k) for k, v in enumerate(cuts[len(halves) :])]
    corners = [[exchange(cut(v, (xodd + k) % 2), "gx", k) for k in (0, 1)] for v in ys]

    side = WINDOW + 2
    rows = sum(box_rows(*c) for c in COLUMNS)
    strip = WINDOW * -(-sz // 16) * 16

    def buffers(slots):
        return [
            pltpu.VMEM((len(COLUMNS), slots, LANES, keys), BF),
            pltpu.VMEM((len(COLUMNS), slots, keys, LANES), BF),
        ] + [pltpu.VMEM((slots, -(-HEADS * box_rows(*c) // 32) * 32, LANES), BF) for c in COLUMNS]

    span = up(max(layout(half_columns(k))[1] for k in range(2)) * (groups - 1), LANES)

    def inner(part, operands):
        return pl.pallas_call(
            functools.partial(inner_kernel, width, len(ys), part),
            out_shape=jax.ShapeDtypeStruct((span if part else up(rows * (groups - 1), LANES), LANES), F32),
            scratch_shapes=[
                pltpu.VMEM((span, LANES), F32),
                pltpu.VMEM((groups // 2, EXT, EXT, ROWS, LANES), F32),
            ]
            + buffers(groups - 1),
            compiler_params=pltpu.CompilerParams(vmem_limit_bytes=20 << 20),
            cost_estimate=pl.CostEstimate(flops=2 * 10**9, transcendentals=0, bytes_accessed=10**6),
        )(*operands)

    def edge(parts):
        def kernel(*refs):
            at = 0
            for r in refs[:-1]:
                refs[-1][at : at + r.shape[0]] = r[:, :, -ROWS:, :]
                at += r.shape[0]

        shape = (sum(p.shape[0] for p in parts),) + (parts[0].shape[1], ROWS, LANES)
        return pl.pallas_call(
            kernel,
            out_shape=jax.ShapeDtypeStruct(shape, BF),
            compiler_params=pltpu.CompilerParams(vmem_limit_bytes=4 << 20),
        )(*parts)

    near = [packed, *xs]
    wide = [v for y, c in zip(ys, corners) for v in (y, *c)]
    if len(ys) == 1:
        early = inner(-1, [geo, *near, *weights])
        rows_first = lax.optimization_barrier((early, *near))
        zs = other_core(edge(rows_first[1:]))
        zcorners = [other_core(edge([y, *c])) for y, c in zip(ys, corners)]
        done = inner(1, [geo, *near, *wide, *weights])
        done = [done, early]
    else:
        zs = other_core(edge(near))
        zcorners = [other_core(edge([y, *c])) for y, c in zip(ys, corners)]
        done = [inner(0, [geo, *near, *wide, *weights])]

    flat = [v for y, c, z in zip(ys, corners, zcorners) for v in (y, *c, z)]
    conv = [pltpu.with_memory_space_constraint(v, pltpu.HBM) for v in (conv_weight, conv_gain[None, :])]
    operands = [geo, *done, *near, zs, *flat, *weights, *conv]
    vmem = pl.BlockSpec(memory_space=pltpu.VMEM)
    hbm = pl.BlockSpec(memory_space=pltpu.HBM)
    return pl.pallas_call(
        functools.partial(last_kernel, width, len(ys)),
        out_shape=jax.ShapeDtypeStruct(volume.shape, volume.dtype),
        in_specs=[vmem] * (len(operands) - 2) + [hbm] * 2,
        scratch_shapes=[
            pltpu.VMEM((2, EXT, EXT, ROWS, LANES), F32),
            pltpu.VMEM((up(2 * rows, LANES), LANES), F32),
            pltpu.VMEM(done[0].shape, F32),
            pltpu.VMEM((side, side, sz + 12, LANES), F32),
            pltpu.VMEM((3 * 4 * HALF, 4 * HALF), BF),
            pltpu.VMEM((-(-WINDOW * strip // LANES) * LANES, LANES), F32),
            pltpu.VMEM(conv[0].shape, conv[0].dtype),
            pltpu.VMEM(conv[1].shape, conv[1].dtype),
            pltpu.SemaphoreType.DMA((2,)),
        ]
        + buffers(2),
        compiler_params=pltpu.CompilerParams(vmem_limit_bytes=26 << 20),
        name="last_windows",
    )(*operands)


def solution(mesh):
    placed = (P(("parts", "gx"), "gy", "gz", None), P(), P(), P(), P(), P(), P(), P())

    return jax.shard_map(
        body,
        mesh=mesh,
        in_specs=placed,
        out_specs=P(("parts", "gx"), "gy", "gz", None),
        check_vma=False,
    )
```

profile of v0, /device:TPU:0, one launch (start us, length us, event | category | flops | bytes accessed | tf_op | source)
XLA Modules:
  0.0 28.5 jit_solution(8266366140150902530)
XLA Ops:
  0.0 5.1 %first_block.1 = (bf16[7,7,16,128]{3,2,1,0:T(8,128)(2,1)S(1)}, bf16[7,4,16,128]{3,2,1,0:T(8,128)(2,1)S(1)}, bf16[4,7,16,128]{3,2,1,0:T(8,128)(2,1)S(1)}, bf16[4,7,16,128]{3,2,1,0:T(8,128)(2,1)S(1)}) custom-call(bf16[7,7,28,48]{3,2,1,0:T(8,128)(2,1)} %refs_0_.1, f32[16,384]{1,0:T(8,128)} %constant.35.clone.refs_1_.geo_ref, bf16[2,48,144]{2,1,0:T(8,128)(2,1)} %refs_9_.1, ...), custom_call_target="tpu_custom_call" | custom-call | tf_op jit(solution)/shard_map/first_block/pallas_call | solution.py:548
  5.2 3.0 %collective-permute-start.2 = (bf16[7,4,16,128]{3,2,1,0:T(8,128)(2,1)S(1)}, bf16[7,4,16,128]{3,2,1,0:T(8,128)(2,1)S(1)}, u32[]{:S(2)}, u32[]{:S(2)}) collective-permute-start(bf16[7,4,16,128]{3,2,1,0:T(8,128)(2,1)S(1)} %get-tuple-element.15), channel_id=1, source_target_pairs={{0,2},{1,3},{2,0},{3,1},{4,6},{5,7},{6,4},{7,5},{8,10},{9,11},{10,... | collective-permute-start | bytes 344072 | tf_op jit(solution)/shard_map/ppermute | solution.py:534
  8.2 1.6 %collective-permute-start = (bf16[4,7,16,128]{3,2,1,0:T(8,128)(2,1)S(1)}, bf16[4,7,16,128]{3,2,1,0:T(8,128)(2,1)S(1)}, u32[]{:S(2)}, u32[]{:S(2)}) collective-permute-start(bf16[4,7,16,128]{3,2,1,0:T(8,128)(2,1)S(1)} %get-tuple-element.13), channel_id=1, source_target_pairs={{0,4},{1,5},{4,0},{5,1},{8,12},{9,13},{12,8},{13,9},{2,6},{3,7},{6... | collective-permute-start | bytes 344072 | tf_op jit(solution)/shard_map/ppermute | solution.py:534
  9.8 0.0 collective-permute-start.1
  9.8 0.0 copy-start.3
  9.8 0.0 copy-start.4
  9.8 1.5 %collective-permute-done.2.refs_3_.refs_0_.refs_5_ = bf16[7,4,16,128]{3,2,1,0:T(8,128)(2,1)S(1)} collective-permute-done((bf16[7,4,16,128]{3,2,1,0:T(8,128)(2,1)S(1)}, bf16[7,4,16,128]{3,2,1,0:T(8,128)(2,1)S(1)}, u32[]{:S(2)}, u32[]{:S(2)}) %collective-permute-start.2) | collective-permute-done | bytes 114720 | tf_op jit(solution)/shard_map/ppermute | solution.py:534
  11.3 0.0 copy-start.5
  11.3 0.1 collective-permute-start.4
  11.4 3.4 %collective-permute-start.3 = (bf16[4,4,16,128]{3,2,1,0:T(8,128)(2,1)S(1)}, bf16[4,4,16,128]{3,2,1,0:T(8,128)(2,1)S(1)}, u32[]{:S(2)}, u32[]{:S(2)}) collective-permute-start(bf16[4,4,16,128]{3,2,1,0:T(8,128)(2,1)S(1)} %get-tuple-element.20), channel_id=1, source_target_pairs={{0,4},{1,5},{4,0},{5,1},{8,12},{9,13},{12,8},{13,9},{2,6},{3,7},{6... | collective-permute-start | bytes 196616 | tf_op jit(solution)/shard_map/ppermute | solution.py:534
  14.8 0.0 collective-permute-done.refs_1_.refs_2_
  14.8 0.0 collective-permute-done.1.refs_2_.refs_3_
  14.8 0.0 copy-done
  14.8 0.0 copy-done.1
  14.8 0.0 copy-done.2
  14.9 3.0 %shard_map.92.refs_0_ = f32[1152,128]{1,0:T(8,128)S(1)} custom-call(f32[16,384]{1,0:T(8,128)S(1)} %copy-done.4, bf16[7,7,16,128]{3,2,1,0:T(8,128)(2,1)S(1)} %get-tuple-element.16.refs_0_.refs_1_, bf16[4,7,16,128]{3,2,1,0:T(8,128)(2,1)S(1)} %collective-permute-done.refs_1_.refs_2_, bf16[4,7,16,128]{3,2,1,0:T(8,128)(2,1)S(1)} %collective-permute-done.1.refs_2_.refs_3_, ...), custom_call_target="tpu_custom_call" | custom-call | flops 2000000000 | bytes 1000000 | tf_op jit(solution)/shard_map/pallas_call | solution.py:595
  17.9 0.1 collective-permute-start.5
  18.0 0.0 collective-permute-done.4.refs_5_.refs_2_.refs_7_
  18.0 0.0 collective-permute-done.3.refs_4_.refs_1_.refs_6_
  18.1 0.5 %collective-permute-start.6 = (bf16[15,4,8,128]{3,2,1,0:T(8,128)(2,1)S(1)}, bf16[15,4,8,128]{3,2,1,0:T(8,128)(2,1)S(1)}, u32[]{:S(2)}, u32[]{:S(2)}) collective-permute-start(bf16[15,4,8,128]{3,2,1,0:T(8,128)(2,1)S(1)} %shard_map.94), channel_id=1, source_target_pairs={{0,1},{1,0},{2,3},{3,2},{4,5},{5,4},{6,7},{7,6},{8,9},{9,8},{10,11... | collective-permute-start | bytes 368648 | tf_op jit(solution)/shard_map/ppermute | solution.py:576
  18.6 2.7 %shard_map.91.inner_ref = f32[1152,128]{1,0:T(8,128)S(1)} custom-call(f32[16,384]{1,0:T(8,128)S(1)} %copy-done.4, bf16[7,7,16,128]{3,2,1,0:T(8,128)(2,1)S(1)} %get-tuple-element.16.refs_0_.refs_1_, bf16[4,7,16,128]{3,2,1,0:T(8,128)(2,1)S(1)} %collective-permute-done.refs_1_.refs_2_, bf16[4,7,16,128]{3,2,1,0:T(8,128)(2,1)S(1)} %collective-permute-done.1.refs_2_.refs_3_, ...), custom_call_target="tpu_custom_call" | custom-call | flops 2000000000 | bytes 1000000 | tf_op jit(solution)/shard_map/pallas_call | solution.py:595
  21.3 0.0 collective-permute-done.6.refs_8_
  21.4 0.0 collective-permute-done.5.refs_4_
  21.4 7.0 %last_windows.1 = bf16[7,7,28,48]{3,2,1,0:T(8,128)(2,1)} custom-call(f32[16,384]{1,0:T(8,128)S(1)} %copy-done.4, f32[1152,128]{1,0:T(8,128)S(1)} %shard_map.91.inner_ref, f32[1152,128]{1,0:T(8,128)S(1)} %shard_map.92.refs_0_, bf16[7,7,16,128]{3,2,1,0:T(8,128)(2,1)S(1)} %get-tuple-element.16.refs_0_.refs_1_, ...), custom_call_target="tpu_custom_call" | custom-call | tf_op jit(solution)/shard_map/last_windows/pallas_call | solution.py:640
  (9 shorter events, 0.1 us)
Async XLA Ops:
  5.2 6.2 %collective-permute-start.2 = (bf16[7,4,16,128]{3,2,1,0:T(8,128)(2,1)S(1)}, bf16[7,4,16,128]{3,2,1,0:T(8,128)(2,1)S(1)}, u32[]{:S(2)}, u32[]{:S(2)}) collective-permute-start(bf16[7,4,16,128]{3,2,1,0:T(8,128)(2,1)S(1)} %get-tuple-element.15), channel_id=1, source_target_pairs={{0,2},{1,3},{2,0},{3,1},{4,6},{5,7},{6,4},{7,5},{8,10},{9,11},{10,... | collective-permute-start | bytes 344072 | tf_op jit(solution)/shard_map/ppermute | solution.py:534
  8.2 6.6 %collective-permute-start = (bf16[4,7,16,128]{3,2,1,0:T(8,128)(2,1)S(1)}, bf16[4,7,16,128]{3,2,1,0:T(8,128)(2,1)S(1)}, u32[]{:S(2)}, u32[]{:S(2)}) collective-permute-start(bf16[4,7,16,128]{3,2,1,0:T(8,128)(2,1)S(1)} %get-tuple-element.13), channel_id=1, source_target_pairs={{0,4},{1,5},{4,0},{5,1},{8,12},{9,13},{12,8},{13,9},{2,6},{3,7},{6... | collective-permute-start | bytes 344072 | tf_op jit(solution)/shard_map/ppermute | solution.py:534
  9.8 5.1 %collective-permute-start.1 = (bf16[4,7,16,128]{3,2,1,0:T(8,128)(2,1)S(1)}, bf16[4,7,16,128]{3,2,1,0:T(8,128)(2,1)S(1)}, u32[]{:S(2)}, u32[]{:S(2)}) collective-permute-start(bf16[4,7,16,128]{3,2,1,0:T(8,128)(2,1)S(1)} %get-tuple-element.14), channel_id=1, source_target_pairs={{0,1},{1,0},{4,8},{5,9},{8,4},{9,5},{12,13},{13,12},{2,3},{3,2},{6... | collective-permute-start | bytes 344072 | tf_op jit(solution)/shard_map/ppermute | solution.py:534
  9.8 5.1 %copy-start = (bf16[2,48,144]{2,1,0:T(8,128)(2,1)S(1)}, bf16[2,48,144]{2,1,0:T(8,128)(2,1)}, u32[]{:S(2)}) copy-start(bf16[2,48,144]{2,1,0:T(8,128)(2,1)} %refs_9_.1) | copy-start | bytes 82948
  9.8 5.1 %copy-start.1 = (bf16[2,48,192]{2,1,0:T(8,128)(2,1)S(1)}, bf16[2,48,192]{2,1,0:T(8,128)(2,1)}, u32[]{:S(2)}) copy-start(bf16[2,48,192]{2,1,0:T(8,128)(2,1)} %refs_11_.1) | copy-start | bytes 110596
  9.8 5.1 %copy-start.2 = (bf16[2,192,48]{1,2,0:T(8,128)(2,1)S(1)}, bf16[2,192,48]{1,2,0:T(8,128)(2,1)}, u32[]{:S(2)}) copy-start(bf16[2,192,48]{1,2,0:T(8,128)(2,1)} %param.13) | copy-start | bytes 110596
  9.8 5.1 %copy-start.3 = (bf16[2,48,48]{2,1,0:T(8,128)(2,1)S(1)}, bf16[2,48,48]{2,1,0:T(8,128)(2,1)}, u32[]{:S(2)}) copy-start(bf16[2,48,48]{2,1,0:T(8,128)(2,1)} %refs_10_.3) | copy-start | bytes 27652
  9.8 5.1 %copy-start.4 = (f32[16,384]{1,0:T(8,128)S(1)}, f32[16,384]{1,0:T(8,128)}, u32[]{:S(2)}) copy-start(f32[16,384]{1,0:T(8,128)} %constant.35.clone.refs_1_.geo_ref) | copy-start | bytes 73732
  11.3 3.5 %copy-start.5 = (f32[2,2,48]{2,1,0:T(2,128)S(1)}, f32[2,2,48]{2,1,0:T(2,128)}, u32[]{:S(2)}) copy-start(f32[2,2,48]{2,1,0:T(2,128)} %refs_13_.1) | copy-start | bytes 2308
  11.3 6.7 %collective-permute-start.4 = (bf16[4,4,16,128]{3,2,1,0:T(8,128)(2,1)S(1)}, bf16[4,4,16,128]{3,2,1,0:T(8,128)(2,1)S(1)}, u32[]{:S(2)}, u32[]{:S(2)}) collective-permute-start(bf16[4,4,16,128]{3,2,1,0:T(8,128)(2,1)S(1)} %get-tuple-element.19), channel_id=1, source_target_pairs={{0,1},{1,0},{4,8},{5,9},{8,4},{9,5},{12,13},{13,12},{2,3},{3,2},{6... | collective-permute-start | bytes 196616 | tf_op jit(solution)/shard_map/ppermute | solution.py:534
  11.4 6.6 %collective-permute-start.3 = (bf16[4,4,16,128]{3,2,1,0:T(8,128)(2,1)S(1)}, bf16[4,4,16,128]{3,2,1,0:T(8,128)(2,1)S(1)}, u32[]{:S(2)}, u32[]{:S(2)}) collective-permute-start(bf16[4,4,16,128]{3,2,1,0:T(8,128)(2,1)S(1)} %get-tuple-element.20), channel_id=1, source_target_pairs={{0,4},{1,5},{4,0},{5,1},{8,12},{9,13},{12,8},{13,9},{2,6},{3,7},{6... | collective-permute-start | bytes 196616 | tf_op jit(solution)/shard_map/ppermute | solution.py:534
  17.9 3.4 %collective-permute-start.5 = (bf16[15,7,8,128]{3,2,1,0:T(8,128)(2,1)S(1)}, bf16[15,7,8,128]{3,2,1,0:T(8,128)(2,1)S(1)}, u32[]{:S(2)}, u32[]{:S(2)}) collective-permute-start(bf16[15,7,8,128]{3,2,1,0:T(8,128)(2,1)S(1)} %shard_map.93), channel_id=1, source_target_pairs={{0,1},{1,0},{2,3},{3,2},{4,5},{5,4},{6,7},{7,6},{8,9},{9,8},{10,11... | collective-permute-start | bytes 645128 | tf_op jit(solution)/shard_map/ppermute | solution.py:576
  18.1 3.3 %collective-permute-start.6 = (bf16[15,4,8,128]{3,2,1,0:T(8,128)(2,1)S(1)}, bf16[15,4,8,128]{3,2,1,0:T(8,128)(2,1)S(1)}, u32[]{:S(2)}, u32[]{:S(2)}) collective-permute-start(bf16[15,4,8,128]{3,2,1,0:T(8,128)(2,1)S(1)} %shard_map.94), channel_id=1, source_target_pairs={{0,1},{1,0},{2,3},{3,2},{4,5},{5,4},{6,7},{7,6},{8,9},{9,8},{10,11... | collective-permute-start | bytes 368648 | tf_op jit(solution)/shard_map/ppermute | solution.py:576
where the time goes:
time: 28.7 us; the launch traced here: 28.5 us
  Pallas kernels  17.9 us (62%)
  starting transfers between devices  8.69 us (30%)
  waiting for transfers between devices  1.54 us (5%)
  between operations  0.33 us (1%)
    ppermute x5, starting transfers between devices, exchange(): return lax.ppermute(v, (axis, 'gz'), pairs)  8.07 us
    pallas_call x1, Pallas kernels, body(): pl.pallas_call(functools.partial(last_kernel, width, len(ys)), out_shape=...  6.99 us
    pallas_call x2, Pallas kernels, inner(): pl.pallas_call(functools.partial(inner_kernel, width, len(ys), part), out...  5.72 us
    pallas_call x1, Pallas kernels, body(): pl.pallas_call(functools.partial(first_kernel, width, len(halves)), out_s...  5.14 us
    ppermute x5, waiting for transfers between devices, exchange(): return lax.ppermute(v, (axis, 'gz'), pairs)  1.54 us
    ppermute x2, starting transfers between devices, other_core(): return lax.ppermute(v, 'gz', [(0, 1), (1, 0)])  0.61 us
  transfers between devices with their start and end apart: 7, of which 1 were waited for; matrix products, arithmetic and copies ran while one was open for 0% of the time, Pallas kernels for 20%

commit v1 on v0

--- a/solution.py
+++ b/solution.py
@@ -212,8 +212,8 @@
     return BOXES[wx][1] * BOXES[wy][1] * ROWS
 
 
-def layout(cols):
-    sizes = [box_rows(*COLUMNS[c]) for c in cols]
+def layout(cols, size=lambda n: n):
+    sizes = [size(box_rows(*COLUMNS[c])) for c in cols]
     return {c: sum(sizes[:i]) for i, c in enumerate(cols)}, sum(sizes)
 
 
@@ -257,7 +257,22 @@
                 ]
 
 
-def window_attention(width, groups, cols, work, start_of, geo_ref, wts, ext, mix, ks, vs, qs, between=None):
+def squeezed(rows):
+    return up(rows // ROWS, 2) // 2 * ROWS
+
+
+def squeeze(rows):
+    n = rows.shape[0] // ROWS
+    if n % 2:
+        rows = jnp.concatenate([rows, jnp.zeros((ROWS, LANES), F32)], 0)
+    m = (n + 1) // 2
+    pairs = rows.reshape(m, 2, ROWS, LANES)
+    even, odd = [pairs[:, k].reshape(m * ROWS, LANES) for k in (0, 1)]
+    low = iota((m * ROWS, LANES), 0) % ROWS < HIGH
+    return jnp.where(low, pltpu.roll(even, m * ROWS - SHIFT, 0), pltpu.roll(odd, 1, 0))
+
+
+def window_attention(width, groups, cols, work, start_of, geo_ref, wts, ext, mix, ks, vs, qs, short=()):
     index, count = position()
     spots = WINDOW * WINDOW
     keys = (spots - 1) * ROWS
@@ -296,9 +311,14 @@
             picked = [
                 vq[ROWS * (WINDOW * x + by) - first : ROWS * (WINDOW * x + by + ny) - first] for x in range(bx, bx + nx)
             ]
-            qs[c][slot] = queries_of(jnp.concatenate(picked, 0), width)
+            picked, residual = jnp.concatenate(picked, 0), chosen
+            if g in short:
+                picked, residual = squeeze(picked), squeeze(residual)
+            queries = queries_of(picked, width)
+            qs[c][slot, 0 : queries.shape[0]] = queries
             start = start_of(g, c)
-            mix[start : start + nq, HALF:] = (chosen if half else pltpu.roll(chosen, HALF, 1))[:, HALF:]
+            residual = residual if half else pltpu.roll(residual, HALF, 1)
+            mix[start : start + residual.shape[0], HALF:] = residual[:, HALF:]
 
     order = [(slab, c) for slab in sorted({w[0] for w in work}) for c in cols]
     ahead = turn(*order[0])
@@ -310,28 +330,51 @@
 
     def job(slot, c):
         n = box_rows(*COLUMNS[c])
+        if work[slot][2] in short:
+            n = squeezed(n)
         start = start_of(work[slot][2], c)
 
         def store(v):
             mix[start : start + n, :HALF] = v[:, :HALF]
 
-        return qs[c].at[slot], ks.at[c, slot], vs.at[c, slot], n, store
-
-    attend([job(slot, c) for slot in range(len(work)) for c in cols], width, between)
+        return qs[c].at[slot, 0 : up(HEADS * n, 32)], ks.at[c, slot], vs.at[c, slot], n, store
+
+    attend([job(slot, c) for slot in range(len(work)) for c in cols], width)
+
+
+def prepare_kernel(wqkv_ref, wproj_ref, wup_ref, wdown_ref, gain_ref, wconv_ref, cgain_ref, *outs):
+    for out, value in zip(outs, block_weights(1, wqkv_ref, wproj_ref, wup_ref, wdown_ref, gain_ref)):
+        out[...] = value
+    cg_ref, wc = outs[7], outs[8]
+    width = wproj_ref.shape[1]
+    diagonal = iota((width, width), 0) == iota((width, width), 1)
+    cg_ref[...] = jnp.sum(jnp.where(diagonal, cgain_ref[...], 0.0), 1, keepdims=True)
+    wc[...] = jnp.zeros(wc.shape, BF)
+    for dx in range(3):
+        total = None
+        for dy in range(3):
+            taps = wconv_ref[9 * dx + 3 * dy : 9 * dx + 3 * dy + 3].reshape(3 * width, width)
+            i, j = iota((width, 4 * HALF), 0), iota((width, 4 * HALF), 1)
+            place = jnp.where(j == i + HALF * dy, 1.0, 0.0).astype(BF)
+            part = mm(taps, place)
+            total = part if total is None else total + part
+        for dz in range(3):
+            at = 4 * HALF * dx + HALF * dz
+            wc[at : at + width] = total[width * dz : width * (dz + 1)].astype(BF)
 
 
 def inner_kernel(width, ypieces, part, geo_ref, *refs):
     pieces = refs[:3] if part < 0 else refs[: 3 * (ypieces + 1)]
     rest = refs[len(pieces) :]
-    wqkv_ref, wproj_ref, wup_ref, wdown_ref, gain_ref, out_ref, mix, ext, ks, vs = rest[:10]
-    qs = rest[10:]
+    wts = [r[...] for r in rest[:7]]
+    out_ref, mix, ext, ks, vs = rest[7:12]
+    qs = rest[12:]
     pairs = pieces[0].shape[2] // ROWS
     work = [(p, half, 1 + 2 * p + half) for p in range(pairs) for half in range(2)][:-1]
     index, _ = position()
     far = WINDOW + HIGH
     xa, xb = [jnp.where(index[0] % 2 == k, far, 0) for k in (0, 1)]
     ys = [jnp.where(index[1] % 2 == k, far, 0) for k in range(2)]
-    wts = block_weights(1, wqkv_ref, wproj_ref, wup_ref, wdown_ref, gain_ref)
     tiles = []
     for k, y in enumerate([HIGH] + ys[: len(pieces) // 3 - 1]):
         for i, x in enumerate((HIGH, xa, xb)):
@@ -374,15 +417,9 @@
         free_ref, *refs = refs
     pieces = refs[: 4 * (ypieces + 1)]
     rest = refs[4 * (ypieces + 1) :]
-    wqkv_ref, wproj_ref, wup_ref, wdown_ref, gain_ref, wconv_hbm, cgain_hbm, out_ref = rest[:8]
-    ext, mix, fed, grid, wc, tot, wconv_ref, cgain_ref, sems, ks, vs = rest[8:19]
-    qs = rest[19:]
-    moves = [
-        pltpu.make_async_copy(wconv_hbm, wconv_ref, sems.at[0]),
-        pltpu.make_async_copy(cgain_hbm, cgain_ref, sems.at[1]),
-    ]
-    for m in moves:
-        m.start()
+    wts = [r[...] for r in rest[:7]]
+    cg_ref, wc, out_ref, ext, mix, fed, grid, tot, ks, vs = rest[7:17]
+    qs = rest[17:]
     nz = out_ref.shape[2]
     pairs = pieces[0].shape[2] // ROWS
     groups = 2 * pairs + 1
@@ -390,7 +427,6 @@
     far = WINDOW + HIGH
     xa, xb = [jnp.where(index[0] % 2 == k, far, 0) for k in (0, 1)]
     ys = [jnp.where(index[1] % 2 == k, far, 0) for k in range(2)]
-    wts = block_weights(1, wqkv_ref, wproj_ref, wup_ref, wdown_ref, gain_ref)
     tiles = []
     for k, y in enumerate([HIGH] + ys[:ypieces]):
         at = 0
@@ -420,17 +456,22 @@
                     at = base + places[c] + ROWS * (x * ny + y)
                     grid[HIGH * wx + x, HIGH * wy + y, WINDOW * g : WINDOW * (g + 1), :] = rows[at : at + WINDOW]
 
-    used = 2 * per
+    places, lowest = layout(cols, squeezed)
+    used = lowest + per
     stop = up(used, LANES)
     mix[used:stop] = jnp.zeros((stop - used, LANES), F32)
     fed[...] = feed_rows(inner_ref, inner_ref.shape[0], wts, width)
     place_all(ext, split, tiles, COLUMNS)
     work = [(0, 1, groups - 1), (1, 1, 0)]
-    start = lambda g, c: (per if g else 0) + offsets[c]
-    window_attention(width, groups, cols, work, start, geo_ref, wts, ext, mix, ks, vs, qs)
+    start = lambda g, c: lowest + offsets[c] if g else places[c]
+    window_attention(width, groups, cols, work, start, geo_ref, wts, ext, mix, ks, vs, qs, (0,))
     out = feed_rows(mix, stop, wts, width)
-    scatter(0, out, 0, cols)
-    scatter(groups - 1, out, per, cols)
+    for c, (wx, wy) in enumerate(COLUMNS):
+        (_, nx), (_, ny) = BOXES[wx], BOXES[wy]
+        for i in range(nx * ny):
+            at = places[c] + HIGH * i
+            grid[HIGH * wx + i // ny, HIGH * wy + i % ny, SHIFT:WINDOW, :] = out[at : at + HIGH]
+    scatter(groups - 1, out, lowest, cols)
     if early:
         for side in range(2):
 
@@ -458,21 +499,6 @@
     clear(index[1] == count[1] - 1, slice(None), slice(last, last + 1))
     clear(index[2] == 0, slice(None), slice(None), slice(SHIFT, HIGH))
     clear(index[2] == count[2] - 1, slice(None), slice(None), slice(HIGH + nz, HIGH + nz + 1))
-
-    for m in moves:
-        m.wait()
-    wc[...] = jnp.zeros(wc.shape, BF)
-    for dx in range(3):
-        total = None
-        for dy in range(3):
-            taps = wconv_ref[9 * dx + 3 * dy : 9 * dx + 3 * dy + 3].reshape(3 * width, width)
-            i, j = iota((width, 4 * HALF), 0), iota((width, 4 * HALF), 1)
-            place = jnp.where(j == i + HALF * dy, 1.0, 0.0).astype(BF)
-            part = mm(taps, place)
-            total = part if total is None else total + part
-        for dz in range(3):
-            at = 4 * HALF * dx + HALF * dz
-            wc[at : at + width] = total[width * dz : width * (dz + 1)].astype(BF)
 
     side = WINDOW + 2
     padded = -(-nz // 16) * 16
@@ -491,9 +517,7 @@
         turned = pltpu.roll(near[padded : (WINDOW + 1) * padded], HALF, 1)
         tot[x * strip : (x + 1) * strip] = near[:strip] + turned + second[2 * padded :]
     tot[WINDOW * strip :] = jnp.zeros((tot.shape[0] - WINDOW * strip, LANES), F32)
-    diagonal = iota((width, width), 0) == iota((width, width), 1)
-    cg = jnp.sum(jnp.where(diagonal, cgain_ref[...], 0.0), 1, keepdims=True)
-    normed = norm_cols(jnp.transpose(tot[...])[:width], cg, width)
+    normed = norm_cols(jnp.transpose(tot[...])[:width], cg_ref[...], width)
     active = jnp.where(normed >= 0.0, normed, 0.01 * normed)
     active = jnp.transpose(jnp.concatenate([active, jnp.zeros((LANES - width, tot.shape[0]), F32)], 0))
     for x in range(WINDOW):
@@ -604,6 +628,26 @@
             cost_estimate=pl.CostEstimate(flops=2 * 10**9, transcendentals=0, bytes_accessed=10**6),
         )(*operands)
 
+    hidden = w_up.shape[2]
+    column = jax.ShapeDtypeStruct((width, 1), F32)
+    ready = pl.pallas_call(
+        prepare_kernel,
+        out_shape=[
+            jax.ShapeDtypeStruct((width, LANES), BF),
+            jax.ShapeDtypeStruct((width, width), BF),
+            column,
+            jax.ShapeDtypeStruct((width, LANES), BF),
+            jax.ShapeDtypeStruct((width, hidden), BF),
+            jax.ShapeDtypeStruct((width, hidden), BF),
+            column,
+            column,
+            jax.ShapeDtypeStruct((3 * 4 * HALF, 4 * HALF), BF),
+        ],
+        compiler_params=pltpu.CompilerParams(vmem_limit_bytes=8 << 20),
+        name="prepare",
+    )(*weights, conv_weight, conv_gain[None, :])
+    block = ready[:7]
+
     def edge(parts):
         def kernel(*refs):
             at = 0
@@ -621,36 +665,28 @@
     near = [packed, *xs]
     wide = [v for y, c in zip(ys, corners) for v in (y, *c)]
     if len(ys) == 1:
-        early = inner(-1, [geo, *near, *weights])
+        early = inner(-1, [geo, *near, *block])
         rows_first = lax.optimization_barrier((early, *near))
         zs = other_core(edge(rows_first[1:]))
         zcorners = [other_core(edge([y, *c])) for y, c in zip(ys, corners)]
-        done = inner(1, [geo, *near, *wide, *weights])
+        done = inner(1, [geo, *near, *wide, *block])
         done = [done, early]
     else:
         zs = other_core(edge(near))
         zcorners = [other_core(edge([y, *c])) for y, c in zip(ys, corners)]
-        done = [inner(0, [geo, *near, *wide, *weights])]
+        done = [inner(0, [geo, *near, *wide, *block])]
 
     flat = [v for y, c, z in zip(ys, corners, zcorners) for v in (y, *c, z)]
-    conv = [pltpu.with_memory_space_constraint(v, pltpu.HBM) for v in (conv_weight, conv_gain[None, :])]
-    operands = [geo, *done, *near, zs, *flat, *weights, *conv]
-    vmem = pl.BlockSpec(memory_space=pltpu.VMEM)
-    hbm = pl.BlockSpec(memory_space=pltpu.HBM)
+    operands = [geo, *done, *near, zs, *flat, *ready]
     return pl.pallas_call(
         functools.partial(last_kernel, width, len(ys)),
         out_shape=jax.ShapeDtypeStruct(volume.shape, volume.dtype),
-        in_specs=[vmem] * (len(operands) - 2) + [hbm] * 2,
         scratch_shapes=[
             pltpu.VMEM((2, EXT, EXT, ROWS, LANES), F32),
-            pltpu.VMEM((up(2 * rows, LANES), LANES), F32),
+            pltpu.VMEM((up(layout(range(len(COLUMNS)), squeezed)[1] + rows, LANES), LANES), F32),
             pltpu.VMEM(done[0].shape, F32),
             pltpu.VMEM((side, side, sz + 12, LANES), F32),
-            pltpu.VMEM((3 * 4 * HALF, 4 * HALF), BF),
             pltpu.VMEM((-(-WINDOW * strip // LANES) * LANES, LANES), F32),
-            pltpu.VMEM(conv[0].shape, conv[0].dtype),
-            pltpu.VMEM(conv[1].shape, conv[1].dtype),
-            pltpu.SemaphoreType.DMA((2,)),
         ]
         + buffers(2),
         compiler_params=pltpu.CompilerParams(vmem_limit_bytes=26 << 20),

time: 28.7 us -> 28 us (0.976)
  waiting for transfers between devices: 1.54 us -> 0.46 us
  local copies, waits for them, and re-layouts: 0.04 us -> 0.73 us
    ppermute x5, waiting for transfers between devices: 1.54 us -> 0.45 us  [exchange(): return lax.ppermute(v, (axis, 'gz'), pairs)]
    unnamed x12 -> x16, local copies, waits for them, and re-layouts: 0.03 us -> 0.72 us
    pallas_call x1, Pallas kernels: 6.99 us -> 6.56 us  [body(): pl.pallas_call(functools.partial(last_kernel, width, len(ys)), out_shape=...]
    pallas_call x0 -> x1, Pallas kernels: none -> 0.36 us  [body(): pl.pallas_call(prepare_kernel, out_shape=[jax.ShapeDtypeStruct((width, LA...]
  transfers between devices with their start and end apart: 7 -> 7, of which waited for: 1 -> 1; matrix products, arithmetic and copies ran while one was open for 0% -> 0% of each run, Pallas kernels for 20% -> 22%
where the time goes in v1:
time: 28 us; the launch traced here: 27.8 us
  Pallas kernels  17.8 us (64%)
  starting transfers between devices  8.7 us (31%)
  local copies, waits for them, and re-layouts  0.73 us (3%)
  waiting for transfers between devices  0.46 us (2%)
    ppermute x5, starting transfers between devices, exchange(): return lax.ppermute(v, (axis, 'gz'), pairs)  8.09 us
    pallas_call x1, Pallas kernels, body(): pl.pallas_call(functools.partial(last_kernel, width, len(ys)), out_shape=...  6.56 us
    pallas_call x2, Pallas kernels, inner(): pl.pallas_call(functools.partial(inner_kernel, width, len(ys), part), out...  5.63 us
    pallas_call x1, Pallas kernels, body(): pl.pallas_call(functools.partial(first_kernel, width, len(halves)), out_s...  5.19 us
    unnamed x16, local copies, waits for them, and re-layouts  0.72 us
    ppermute x2, starting transfers between devices, other_core(): return lax.ppermute(v, 'gz', [(0, 1), (1, 0)])  0.61 us
  transfers between devices with their start and end apart: 7, of which 1 were waited for; matrix products, arithmetic and copies ran while one was open for 0% of the time, Pallas kernels for 22%

profile of v1, /device:TPU:0, one launch (start us, length us, event | category | flops | bytes accessed | tf_op | source)
XLA Modules:
  0.0 27.8 jit_solution(18080276842593376720)
XLA Ops:
  0.0 5.2 %first_block.1 = (bf16[7,7,16,128]{3,2,1,0:T(8,128)(2,1)S(1)}, bf16[7,4,16,128]{3,2,1,0:T(8,128)(2,1)S(1)}, bf16[4,7,16,128]{3,2,1,0:T(8,128)(2,1)S(1)}, bf16[4,7,16,128]{3,2,1,0:T(8,128)(2,1)S(1)}) custom-call(bf16[7,7,28,48]{3,2,1,0:T(8,128)(2,1)} %refs_0_.1, f32[16,384]{1,0:T(8,128)} %constant.35.clone.refs_1_.geo_ref, bf16[2,48,144]{2,1,0:T(8,128)(2,1)} %wqkv_ref.1, ...), custom_call_target="tpu_custom_call" | custom-call | tf_op jit(solution)/shard_map/first_block/pallas_call | solution.py:572
  5.2 0.0 copy-start.1
  5.2 3.0 %collective-permute-start.2 = (bf16[7,4,16,128]{3,2,1,0:T(8,128)(2,1)S(1)}, bf16[7,4,16,128]{3,2,1,0:T(8,128)(2,1)S(1)}, u32[]{:S(2)}, u32[]{:S(2)}) collective-permute-start(bf16[7,4,16,128]{3,2,1,0:T(8,128)(2,1)S(1)} %get-tuple-element.24), channel_id=1, source_target_pairs={{0,2},{1,3},{2,0},{3,1},{4,6},{5,7},{6,4},{7,5},{8,10},{9,11},{10,... | collective-permute-start | bytes 344072 | tf_op jit(solution)/shard_map/ppermute | solution.py:558
  8.3 1.6 %collective-permute-start = (bf16[4,7,16,128]{3,2,1,0:T(8,128)(2,1)S(1)}, bf16[4,7,16,128]{3,2,1,0:T(8,128)(2,1)S(1)}, u32[]{:S(2)}, u32[]{:S(2)}) collective-permute-start(bf16[4,7,16,128]{3,2,1,0:T(8,128)(2,1)S(1)} %get-tuple-element.22), channel_id=1, source_target_pairs={{0,4},{1,5},{4,0},{5,1},{8,12},{9,13},{12,8},{13,9},{2,6},{3,7},{6... | collective-permute-start | bytes 344072 | tf_op jit(solution)/shard_map/ppermute | solution.py:558
  9.8 0.0 collective-permute-start.1
  9.8 0.0 copy-done
  9.9 0.0 copy-done.2
  9.9 0.7 %copy-done.5 = bf16[2,48,48]{2,1,0:T(8,128)(2,1)S(1)} copy-done((bf16[2,48,48]{2,1,0:T(8,128)(2,1)S(1)}, bf16[2,48,48]{2,1,0:T(8,128)(2,1)}, u32[]{:S(2)}) %copy-start.5) | copy-done | bytes 9240
  10.6 0.4 %prepare.1 = (bf16[48,128]{1,0:T(8,128)(2,1)S(1)}, bf16[48,48]{1,0:T(8,128)(2,1)S(1)}, f32[48,1]{1,0:T(8,128)S(1)}, bf16[48,128]{1,0:T(8,128)(2,1)S(1)}, bf16[48...) custom-call(bf16[2,48,144]{2,1,0:T(8,128)(2,1)S(1)} %copy-done.1, ...), custom_call_target="tpu_custom_call" | custom-call | tf_op jit(solution)/shard_map/prepare/pallas_call | solution.py:633
  10.9 0.0 copy-start.4
  11.0 0.4 %collective-permute-done.2.refs_3_.refs_0_.refs_5_ = bf16[7,4,16,128]{3,2,1,0:T(8,128)(2,1)S(1)} collective-permute-done((bf16[7,4,16,128]{3,2,1,0:T(8,128)(2,1)S(1)}, bf16[7,4,16,128]{3,2,1,0:T(8,128)(2,1)S(1)}, u32[]{:S(2)}, u32[]{:S(2)}) %collective-permute-start.2) | collective-permute-done | bytes 114720 | tf_op jit(solution)/shard_map/ppermute | solution.py:558
  11.4 0.2 collective-permute-start.4
  11.6 3.3 %collective-permute-start.3 = (bf16[4,4,16,128]{3,2,1,0:T(8,128)(2,1)S(1)}, bf16[4,4,16,128]{3,2,1,0:T(8,128)(2,1)S(1)}, u32[]{:S(2)}, u32[]{:S(2)}) collective-permute-start(bf16[4,4,16,128]{3,2,1,0:T(8,128)(2,1)S(1)} %get-tuple-element.38), channel_id=1, source_target_pairs={{0,4},{1,5},{4,0},{5,1},{8,12},{9,13},{12,8},{13,9},{2,6},{3,7},{6... | collective-permute-start | bytes 196616 | tf_op jit(solution)/shard_map/ppermute | solution.py:558
  14.9 0.0 collective-permute-done.refs_1_.refs_2_
  14.9 0.0 collective-permute-done.1.refs_2_.refs_3_
  14.9 3.0 %shard_map.92.refs_0_ = f32[1152,128]{1,0:T(8,128)S(1)} custom-call(f32[16,384]{1,0:T(8,128)S(1)} %copy-done.4, bf16[7,7,16,128]{3,2,1,0:T(8,128)(2,1)S(1)} %get-tuple-element.32.refs_0_.refs_1_, bf16[4,7,16,128]{3,2,1,0:T(8,128)(2,1)S(1)} %collective-permute-done.refs_1_.refs_2_, bf16[4,7,16,128]{3,2,1,0:T(8,128)(2,1)S(1)} %collective-permute-done.1.refs_2_.refs_3_, ...), custom_call_target="tpu_custom_call" | custom-call | flops 2000000000 | bytes 1000000 | tf_op jit(solution)/shard_map/pallas_call | solution.py:619
  17.9 0.1 collective-permute-start.5
  18.0 0.0 collective-permute-done.4.refs_5_.refs_2_.refs_7_
  18.0 0.0 collective-permute-done.3.refs_4_.refs_1_.refs_6_
  18.0 0.5 %collective-permute-start.6 = (bf16[15,4,8,128]{3,2,1,0:T(8,128)(2,1)S(1)}, bf16[15,4,8,128]{3,2,1,0:T(8,128)(2,1)S(1)}, u32[]{:S(2)}, u32[]{:S(2)}) collective-permute-start(bf16[15,4,8,128]{3,2,1,0:T(8,128)(2,1)S(1)} %shard_map.94), channel_id=1, source_target_pairs={{0,1},{1,0},{2,3},{3,2},{4,5},{5,4},{6,7},{7,6},{8,9},{9,8},{10,11... | collective-permute-start | bytes 368648 | tf_op jit(solution)/shard_map/ppermute | solution.py:600
  18.6 2.7 %shard_map.91.inner_ref = f32[1152,128]{1,0:T(8,128)S(1)} custom-call(f32[16,384]{1,0:T(8,128)S(1)} %copy-done.4, bf16[7,7,16,128]{3,2,1,0:T(8,128)(2,1)S(1)} %get-tuple-element.32.refs_0_.refs_1_, bf16[4,7,16,128]{3,2,1,0:T(8,128)(2,1)S(1)} %collective-permute-done.refs_1_.refs_2_, bf16[4,7,16,128]{3,2,1,0:T(8,128)(2,1)S(1)} %collective-permute-done.1.refs_2_.refs_3_, ...), custom_call_target="tpu_custom_call" | custom-call | flops 2000000000 | bytes 1000000 | tf_op jit(solution)/shard_map/pallas_call | solution.py:619
  21.3 0.0 collective-permute-done.6.refs_8_
  21.3 0.0 collective-permute-done.5.refs_4_
  21.3 6.6 %last_windows.1 = bf16[7,7,28,48]{3,2,1,0:T(8,128)(2,1)} custom-call(f32[16,384]{1,0:T(8,128)S(1)} %copy-done.4, f32[1152,128]{1,0:T(8,128)S(1)} %shard_map.91.inner_ref, f32[1152,128]{1,0:T(8,128)S(1)} %shard_map.92.refs_0_, bf16[7,7,16,128]{3,2,1,0:T(8,128)(2,1)S(1)} %get-tuple-element.32.refs_0_.refs_1_, ...), custom_call_target="tpu_custom_call" | custom-call | tf_op jit(solution)/shard_map/last_windows/pallas_call | solution.py:681
  (14 shorter events, 0.1 us)
Async XLA Ops:
  0.0 9.8 %copy-start = (bf16[27,48,48]{2,1,0:T(8,128)(2,1)S(1)}, bf16[27,48,48]{2,1,0:T(8,128)(2,1)}, u32[]{:S(2)}) copy-start(bf16[27,48,48]{2,1,0:T(8,128)(2,1)} %wconv_ref.1) | copy-start | bytes 373252
  0.0 9.9 %copy-start.2 = (bf16[2,48,192]{2,1,0:T(8,128)(2,1)S(1)}, bf16[2,48,192]{2,1,0:T(8,128)(2,1)}, u32[]{:S(2)}) copy-start(bf16[2,48,192]{2,1,0:T(8,128)(2,1)} %wup_ref.1) | copy-start | bytes 110596
  0.0 9.9 %copy-start.3 = (bf16[2,192,48]{1,2,0:T(8,128)(2,1)S(1)}, bf16[2,192,48]{1,2,0:T(8,128)(2,1)}, u32[]{:S(2)}) copy-start(bf16[2,192,48]{1,2,0:T(8,128)(2,1)} %param.13) | copy-start | bytes 110596
  5.2 4.7 %copy-start.1 = (bf16[2,48,144]{2,1,0:T(8,128)(2,1)S(1)}, bf16[2,48,144]{2,1,0:T(8,128)(2,1)}, u32[]{:S(2)}) copy-start(bf16[2,48,144]{2,1,0:T(8,128)(2,1)} %wqkv_ref.1) | copy-start | bytes 82948
  5.2 6.2 %collective-permute-start.2 = (bf16[7,4,16,128]{3,2,1,0:T(8,128)(2,1)S(1)}, bf16[7,4,16,128]{3,2,1,0:T(8,128)(2,1)S(1)}, u32[]{:S(2)}, u32[]{:S(2)}) collective-permute-start(bf16[7,4,16,128]{3,2,1,0:T(8,128)(2,1)S(1)} %get-tuple-element.24), channel_id=1, source_target_pairs={{0,2},{1,3},{2,0},{3,1},{4,6},{5,7},{6,4},{7,5},{8,10},{9,11},{10,... | collective-permute-start | bytes 344072 | tf_op jit(solution)/shard_map/ppermute | solution.py:558
  8.3 6.6 %collective-permute-start = (bf16[4,7,16,128]{3,2,1,0:T(8,128)(2,1)S(1)}, bf16[4,7,16,128]{3,2,1,0:T(8,128)(2,1)S(1)}, u32[]{:S(2)}, u32[]{:S(2)}) collective-permute-start(bf16[4,7,16,128]{3,2,1,0:T(8,128)(2,1)S(1)} %get-tuple-element.22), channel_id=1, source_target_pairs={{0,4},{1,5},{4,0},{5,1},{8,12},{9,13},{12,8},{13,9},{2,6},{3,7},{6... | collective-permute-start | bytes 344072 | tf_op jit(solution)/shard_map/ppermute | solution.py:558
  9.8 5.1 %collective-permute-start.1 = (bf16[4,7,16,128]{3,2,1,0:T(8,128)(2,1)S(1)}, bf16[4,7,16,128]{3,2,1,0:T(8,128)(2,1)S(1)}, u32[]{:S(2)}, u32[]{:S(2)}) collective-permute-start(bf16[4,7,16,128]{3,2,1,0:T(8,128)(2,1)S(1)} %get-tuple-element.23), channel_id=1, source_target_pairs={{0,1},{1,0},{4,8},{5,9},{8,4},{9,5},{12,13},{13,12},{2,3},{3,2},{6... | collective-permute-start | bytes 344072 | tf_op jit(solution)/shard_map/ppermute | solution.py:558
  9.8 0.7 %copy-start.5 = (bf16[2,48,48]{2,1,0:T(8,128)(2,1)S(1)}, bf16[2,48,48]{2,1,0:T(8,128)(2,1)}, u32[]{:S(2)}) copy-start(bf16[2,48,48]{2,1,0:T(8,128)(2,1)} %wproj_ref.1) | copy-start | bytes 27652
  9.8 0.7 %copy-start.6 = (f32[2,2,48]{2,1,0:T(2,128)S(1)}, f32[2,2,48]{2,1,0:T(2,128)}, u32[]{:S(2)}) copy-start(f32[2,2,48]{2,1,0:T(2,128)} %gain_ref.1) | copy-start | bytes 2308
  9.8 0.7 %copy-start.7 = (f32[48]{0:T(128)S(1)}, f32[48]{0:T(128)}, u32[]{:S(2)}) copy-start(f32[48]{0:T(128)} %param.16) | copy-start | bytes 580
  10.9 4.0 %copy-start.4 = (f32[16,384]{1,0:T(8,128)S(1)}, f32[16,384]{1,0:T(8,128)}, u32[]{:S(2)}) copy-start(f32[16,384]{1,0:T(8,128)} %constant.35.clone.refs_1_.geo_ref) | copy-start | bytes 73732
  11.4 6.6 %collective-permute-start.4 = (bf16[4,4,16,128]{3,2,1,0:T(8,128)(2,1)S(1)}, bf16[4,4,16,128]{3,2,1,0:T(8,128)(2,1)S(1)}, u32[]{:S(2)}, u32[]{:S(2)}) collective-permute-start(bf16[4,4,16,128]{3,2,1,0:T(8,128)(2,1)S(1)} %get-tuple-element.37), channel_id=1, source_target_pairs={{0,1},{1,0},{4,8},{5,9},{8,4},{9,5},{12,13},{13,12},{2,3},{3,2},{6... | collective-permute-start | bytes 196616 | tf_op jit(solution)/shard_map/ppermute | solution.py:558
  11.6 6.4 %collective-permute-start.3 = (bf16[4,4,16,128]{3,2,1,0:T(8,128)(2,1)S(1)}, bf16[4,4,16,128]{3,2,1,0:T(8,128)(2,1)S(1)}, u32[]{:S(2)}, u32[]{:S(2)}) collective-permute-start(bf16[4,4,16,128]{3,2,1,0:T(8,128)(2,1)S(1)} %get-tuple-element.38), channel_id=1, source_target_pairs={{0,4},{1,5},{4,0},{5,1},{8,12},{9,13},{12,8},{13,9},{2,6},{3,7},{6... | collective-permute-start | bytes 196616 | tf_op jit(solution)/shard_map/ppermute | solution.py:558
  17.9 3.4 %collective-permute-start.5 = (bf16[15,7,8,128]{3,2,1,0:T(8,128)(2,1)S(1)}, bf16[15,7,8,128]{3,2,1,0:T(8,128)(2,1)S(1)}, u32[]{:S(2)}, u32[]{:S(2)}) collective-permute-start(bf16[15,7,8,128]{3,2,1,0:T(8,128)(2,1)S(1)} %shard_map.93), channel_id=1, source_target_pairs={{0,1},{1,0},{2,3},{3,2},{4,5},{5,4},{6,7},{7,6},{8,9},{9,8},{10,11... | collective-permute-start | bytes 645128 | tf_op jit(solution)/shard_map/ppermute | solution.py:600
  18.0 3.2 %collective-permute-start.6 = (bf16[15,4,8,128]{3,2,1,0:T(8,128)(2,1)S(1)}, bf16[15,4,8,128]{3,2,1,0:T(8,128)(2,1)S(1)}, u32[]{:S(2)}, u32[]{:S(2)}) collective-permute-start(bf16[15,4,8,128]{3,2,1,0:T(8,128)(2,1)S(1)} %shard_map.94), channel_id=1, source_target_pairs={{0,1},{1,0},{2,3},{3,2},{4,5},{5,4},{6,7},{7,6},{8,9},{9,8},{10,11... | collective-permute-start | bytes 368648 | tf_op jit(solution)/shard_map/ppermute | solution.py:600

commit v2 on v0

--- a/solution.py
+++ b/solution.py
@@ -94,7 +94,7 @@
     return jnp.concatenate(parts, 0).astype(BF)
 
 
-def attend(jobs, width, between=None):
+def attend(jobs, width):
     head_dim = width // HEADS
     jobs = list(jobs)
     ahead = mm(jobs[0][0][...], jobs[0][1][...])
@@ -102,8 +102,6 @@
         scores = ahead
         if i + 1 < len(jobs):
             ahead = mm(jobs[i + 1][0][...], jobs[i + 1][1][...])
-        if between is not None:
-            between(i)
         top = jnp.max(scores, -1, keepdims=True)
         weights = jnp.exp(scores - top).astype(BF)
         out = mm(weights, values[...])
@@ -212,8 +210,8 @@
     return BOXES[wx][1] * BOXES[wy][1] * ROWS
 
 
-def layout(cols):
-    sizes = [box_rows(*COLUMNS[c]) for c in cols]
+def layout(cols, size=lambda n: n):
+    sizes = [size(box_rows(*COLUMNS[c])) for c in cols]
     return {c: sum(sizes[:i]) for i, c in enumerate(cols)}, sum(sizes)
 
 
@@ -257,7 +255,22 @@
                 ]
 
 
-def window_attention(width, groups, cols, work, start_of, geo_ref, wts, ext, mix, ks, vs, qs, between=None):
+def squeezed(rows):
+    return up(rows // ROWS, 2) // 2 * ROWS
+
+
+def squeeze(rows):
+    n = rows.shape[0] // ROWS
+    if n % 2:
+        rows = jnp.concatenate([rows, jnp.zeros((ROWS, LANES), F32)], 0)
+    m = (n + 1) // 2
+    pairs = rows.reshape(m, 2, ROWS, LANES)
+    even, odd = [pairs[:, k].reshape(m * ROWS, LANES) for k in (0, 1)]
+    low = iota((m * ROWS, LANES), 0) % ROWS < HIGH
+    return jnp.where(low, pltpu.roll(even, m * ROWS - SHIFT, 0), pltpu.roll(odd, 1, 0))
+
+
+def window_attention(width, groups, cols, work, start_of, geo_ref, wts, ext, mix, ks, vs, qs, short=()):
     index, count = position()
     spots = WINDOW * WINDOW
     keys = (spots - 1) * ROWS
@@ -296,9 +309,14 @@
             picked = [
                 vq[ROWS * (WINDOW * x + by) - first : ROWS * (WINDOW * x + by + ny) - first] for x in range(bx, bx + nx)
             ]
-            qs[c][slot] = queries_of(jnp.concatenate(picked, 0), width)
+            picked, residual = jnp.concatenate(picked, 0), chosen
+            if g in short:
+                picked, residual = squeeze(picked), squeeze(residual)
+            queries = queries_of(picked, width)
+            qs[c][slot, 0 : queries.shape[0]] = queries
             start = start_of(g, c)
-            mix[start : start + nq, HALF:] = (chosen if half else pltpu.roll(chosen, HALF, 1))[:, HALF:]
+            residual = residual if half else pltpu.roll(residual, HALF, 1)
+            mix[start : start + residual.shape[0], HALF:] = residual[:, HALF:]
 
     order = [(slab, c) for slab in sorted({w[0] for w in work}) for c in cols]
     ahead = turn(*order[0])
@@ -310,14 +328,16 @@
 
     def job(slot, c):
         n = box_rows(*COLUMNS[c])
+        if work[slot][2] in short:
+            n = squeezed(n)
         start = start_of(work[slot][2], c)
 
         def store(v):
             mix[start : start + n, :HALF] = v[:, :HALF]
 
-        return qs[c].at[slot], ks.at[c, slot], vs.at[c, slot], n, store
-
-    attend([job(slot, c) for slot in range(len(work)) for c in cols], width, between)
+        return qs[c].at[slot, 0 : up(HEADS * n, 32)], ks.at[c, slot], vs.at[c, slot], n, store
+
+    attend([job(slot, c) for slot in range(len(work)) for c in cols], width)
 
 
 def inner_kernel(width, ypieces, part, geo_ref, *refs):
@@ -420,17 +440,22 @@
                     at = base + places[c] + ROWS * (x * ny + y)
                     grid[HIGH * wx + x, HIGH * wy + y, WINDOW * g : WINDOW * (g + 1), :] = rows[at : at + WINDOW]
 
-    used = 2 * per
+    places, lowest = layout(cols, squeezed)
+    used = lowest + per
     stop = up(used, LANES)
     mix[used:stop] = jnp.zeros((stop - used, LANES), F32)
     fed[...] = feed_rows(inner_ref, inner_ref.shape[0], wts, width)
     place_all(ext, split, tiles, COLUMNS)
     work = [(0, 1, groups - 1), (1, 1, 0)]
-    start = lambda g, c: (per if g else 0) + offsets[c]
-    window_attention(width, groups, cols, work, start, geo_ref, wts, ext, mix, ks, vs, qs)
+    start = lambda g, c: lowest + offsets[c] if g else places[c]
+    window_attention(width, groups, cols, work, start, geo_ref, wts, ext, mix, ks, vs, qs, (0,))
     out = feed_rows(mix, stop, wts, width)
-    scatter(0, out, 0, cols)
-    scatter(groups - 1, out, per, cols)
+    for c, (wx, wy) in enumerate(COLUMNS):
+        (_, nx), (_, ny) = BOXES[wx], BOXES[wy]
+        for i in range(nx * ny):
+            at = places[c] + HIGH * i
+            grid[HIGH * wx + i // ny, HIGH * wy + i % ny, SHIFT:WINDOW, :] = out[at : at + HIGH]
+    scatter(groups - 1, out, lowest, cols)
     if early:
         for side in range(2):
 
@@ -643,7 +668,7 @@
         in_specs=[vmem] * (len(operands) - 2) + [hbm] * 2,
         scratch_shapes=[
             pltpu.VMEM((2, EXT, EXT, ROWS, LANES), F32),
-            pltpu.VMEM((up(2 * rows, LANES), LANES), F32),
+            pltpu.VMEM((up(layout(range(len(COLUMNS)), squeezed)[1] + rows, LANES), LANES), F32),
             pltpu.VMEM(done[0].shape, F32),
             pltpu.VMEM((side, side, sz + 12, LANES), F32),
             pltpu.VMEM((3 * 4 * HALF, 4 * HALF), BF),

time: 28.7 us -> 28.4 us (0.990)
  Pallas kernels: 17.9 us -> 17.6 us
    pallas_call x1, Pallas kernels: 6.99 us -> 6.68 us  [body(): pl.pallas_call(functools.partial(last_kernel, width, len(ys)), out_shape=...]
  transfers between devices with their start and end apart: 7 -> 7, of which waited for: 1 -> 1; matrix products, arithmetic and copies ran while one was open for 0% -> 0% of each run, Pallas kernels for 20% -> 21%
where the time goes in v2:
time: 28.4 us; the launch traced here: 28.2 us
  Pallas kernels  17.6 us (62%)
  starting transfers between devices  8.69 us (31%)
  waiting for transfers between devices  1.54 us (5%)
  between operations  0.33 us (1%)
    ppermute x5, starting transfers between devices, exchange(): return lax.ppermute(v, (axis, 'gz'), pairs)  8.07 us
    pallas_call x1, Pallas kernels, body(): pl.pallas_call(functools.partial(last_kernel, width, len(ys)), out_shape=...  6.68 us
    pallas_call x2, Pallas kernels, inner(): pl.pallas_call(functools.partial(inner_kernel, width, len(ys), part), out...  5.72 us
    pallas_call x1, Pallas kernels, body(): pl.pallas_call(functools.partial(first_kernel, width, len(halves)), out_s...  5.14 us
    ppermute x5, waiting for transfers between devices, exchange(): return lax.ppermute(v, (axis, 'gz'), pairs)  1.54 us
    ppermute x2, starting transfers between devices, other_core(): return lax.ppermute(v, 'gz', [(0, 1), (1, 0)])  0.61 us
  transfers between devices with their start and end apart: 7, of which 1 were waited for; matrix products, arithmetic and copies ran while one was open for 0% of the time, Pallas kernels for 21%

profile of v2, /device:TPU:0, one launch (start us, length us, event | category | flops | bytes accessed | tf_op | source)
XLA Modules:
  0.0 28.2 jit_solution(2607073825436568918)
XLA Ops:
  0.0 5.1 %first_block.1 = (bf16[7,7,16,128]{3,2,1,0:T(8,128)(2,1)S(1)}, bf16[7,4,16,128]{3,2,1,0:T(8,128)(2,1)S(1)}, bf16[4,7,16,128]{3,2,1,0:T(8,128)(2,1)S(1)}, bf16[4,7,16,128]{3,2,1,0:T(8,128)(2,1)S(1)}) custom-call(bf16[7,7,28,48]{3,2,1,0:T(8,128)(2,1)} %refs_0_.1, f32[16,384]{1,0:T(8,128)} %constant.35.clone.refs_1_.geo_ref, bf16[2,48,144]{2,1,0:T(8,128)(2,1)} %refs_9_.1, ...), custom_call_target="tpu_custom_call" | custom-call | tf_op jit(solution)/shard_map/first_block/pallas_call | solution.py:573
  5.2 3.0 %collective-permute-start.2 = (bf16[7,4,16,128]{3,2,1,0:T(8,128)(2,1)S(1)}, bf16[7,4,16,128]{3,2,1,0:T(8,128)(2,1)S(1)}, u32[]{:S(2)}, u32[]{:S(2)}) collective-permute-start(bf16[7,4,16,128]{3,2,1,0:T(8,128)(2,1)S(1)} %get-tuple-element.15), channel_id=1, source_target_pairs={{0,2},{1,3},{2,0},{3,1},{4,6},{5,7},{6,4},{7,5},{8,10},{9,11},{10,... | collective-permute-start | bytes 344072 | tf_op jit(solution)/shard_map/ppermute | solution.py:559
  8.2 1.6 %collective-permute-start = (bf16[4,7,16,128]{3,2,1,0:T(8,128)(2,1)S(1)}, bf16[4,7,16,128]{3,2,1,0:T(8,128)(2,1)S(1)}, u32[]{:S(2)}, u32[]{:S(2)}) collective-permute-start(bf16[4,7,16,128]{3,2,1,0:T(8,128)(2,1)S(1)} %get-tuple-element.13), channel_id=1, source_target_pairs={{0,4},{1,5},{4,0},{5,1},{8,12},{9,13},{12,8},{13,9},{2,6},{3,7},{6... | collective-permute-start | bytes 344072 | tf_op jit(solution)/shard_map/ppermute | solution.py:559
  9.8 0.0 collective-permute-start.1
  9.8 0.0 copy-start.3
  9.8 0.0 copy-start.4
  9.8 1.5 %collective-permute-done.2.refs_3_.refs_0_.refs_5_ = bf16[7,4,16,128]{3,2,1,0:T(8,128)(2,1)S(1)} collective-permute-done((bf16[7,4,16,128]{3,2,1,0:T(8,128)(2,1)S(1)}, bf16[7,4,16,128]{3,2,1,0:T(8,128)(2,1)S(1)}, u32[]{:S(2)}, u32[]{:S(2)}) %collective-permute-start.2) | collective-permute-done | bytes 114720 | tf_op jit(solution)/shard_map/ppermute | solution.py:559
  11.3 0.0 copy-start.5
  11.3 0.1 collective-permute-start.4
  11.4 3.4 %collective-permute-start.3 = (bf16[4,4,16,128]{3,2,1,0:T(8,128)(2,1)S(1)}, bf16[4,4,16,128]{3,2,1,0:T(8,128)(2,1)S(1)}, u32[]{:S(2)}, u32[]{:S(2)}) collective-permute-start(bf16[4,4,16,128]{3,2,1,0:T(8,128)(2,1)S(1)} %get-tuple-element.20), channel_id=1, source_target_pairs={{0,4},{1,5},{4,0},{5,1},{8,12},{9,13},{12,8},{13,9},{2,6},{3,7},{6... | collective-permute-start | bytes 196616 | tf_op jit(solution)/shard_map/ppermute | solution.py:559
  14.8 0.0 collective-permute-done.refs_1_.refs_2_
  14.8 0.0 collective-permute-done.1.refs_2_.refs_3_
  14.8 0.0 copy-done
  14.8 0.0 copy-done.1
  14.8 0.0 copy-done.2
  14.9 3.0 %shard_map.92.refs_0_ = f32[1152,128]{1,0:T(8,128)S(1)} custom-call(f32[16,384]{1,0:T(8,128)S(1)} %copy-done.4, bf16[7,7,16,128]{3,2,1,0:T(8,128)(2,1)S(1)} %get-tuple-element.16.refs_0_.refs_1_, bf16[4,7,16,128]{3,2,1,0:T(8,128)(2,1)S(1)} %collective-permute-done.refs_1_.refs_2_, bf16[4,7,16,128]{3,2,1,0:T(8,128)(2,1)S(1)} %collective-permute-done.1.refs_2_.refs_3_, ...), custom_call_target="tpu_custom_call" | custom-call | flops 2000000000 | bytes 1000000 | tf_op jit(solution)/shard_map/pallas_call | solution.py:620
  17.9 0.1 collective-permute-start.5
  18.0 0.0 collective-permute-done.4.refs_5_.refs_2_.refs_7_
  18.0 0.0 collective-permute-done.3.refs_4_.refs_1_.refs_6_
  18.1 0.5 %collective-permute-start.6 = (bf16[15,4,8,128]{3,2,1,0:T(8,128)(2,1)S(1)}, bf16[15,4,8,128]{3,2,1,0:T(8,128)(2,1)S(1)}, u32[]{:S(2)}, u32[]{:S(2)}) collective-permute-start(bf16[15,4,8,128]{3,2,1,0:T(8,128)(2,1)S(1)} %shard_map.94), channel_id=1, source_target_pairs={{0,1},{1,0},{2,3},{3,2},{4,5},{5,4},{6,7},{7,6},{8,9},{9,8},{10,11... | collective-permute-start | bytes 368648 | tf_op jit(solution)/shard_map/ppermute | solution.py:601
  18.6 2.7 %shard_map.91.inner_ref = f32[1152,128]{1,0:T(8,128)S(1)} custom-call(f32[16,384]{1,0:T(8,128)S(1)} %copy-done.4, bf16[7,7,16,128]{3,2,1,0:T(8,128)(2,1)S(1)} %get-tuple-element.16.refs_0_.refs_1_, bf16[4,7,16,128]{3,2,1,0:T(8,128)(2,1)S(1)} %collective-permute-done.refs_1_.refs_2_, bf16[4,7,16,128]{3,2,1,0:T(8,128)(2,1)S(1)} %collective-permute-done.1.refs_2_.refs_3_, ...), custom_call_target="tpu_custom_call" | custom-call | flops 2000000000 | bytes 1000000 | tf_op jit(solution)/shard_map/pallas_call | solution.py:620
  21.3 0.0 collective-permute-done.6.refs_8_
  21.4 0.0 collective-permute-done.5.refs_4_
  21.4 6.7 %last_windows.1 = bf16[7,7,28,48]{3,2,1,0:T(8,128)(2,1)} custom-call(f32[16,384]{1,0:T(8,128)S(1)} %copy-done.4, f32[1152,128]{1,0:T(8,128)S(1)} %shard_map.91.inner_ref, f32[1152,128]{1,0:T(8,128)S(1)} %shard_map.92.refs_0_, bf16[7,7,16,128]{3,2,1,0:T(8,128)(2,1)S(1)} %get-tuple-element.16.refs_0_.refs_1_, ...), custom_call_target="tpu_custom_call" | custom-call | tf_op jit(solution)/shard_map/last_windows/pallas_call | solution.py:665
  (9 shorter events, 0.1 us)
Async XLA Ops:
  5.2 6.2 %collective-permute-start.2 = (bf16[7,4,16,128]{3,2,1,0:T(8,128)(2,1)S(1)}, bf16[7,4,16,128]{3,2,1,0:T(8,128)(2,1)S(1)}, u32[]{:S(2)}, u32[]{:S(2)}) collective-permute-start(bf16[7,4,16,128]{3,2,1,0:T(8,128)(2,1)S(1)} %get-tuple-element.15), channel_id=1, source_target_pairs={{0,2},{1,3},{2,0},{3,1},{4,6},{5,7},{6,4},{7,5},{8,10},{9,11},{10,... | collective-permute-start | bytes 344072 | tf_op jit(solution)/shard_map/ppermute | solution.py:559
  8.2 6.6 %collective-permute-start = (bf16[4,7,16,128]{3,2,1,0:T(8,128)(2,1)S(1)}, bf16[4,7,16,128]{3,2,1,0:T(8,128)(2,1)S(1)}, u32[]{:S(2)}, u32[]{:S(2)}) collective-permute-start(bf16[4,7,16,128]{3,2,1,0:T(8,128)(2,1)S(1)} %get-tuple-element.13), channel_id=1, source_target_pairs={{0,4},{1,5},{4,0},{5,1},{8,12},{9,13},{12,8},{13,9},{2,6},{3,7},{6... | collective-permute-start | bytes 344072 | tf_op jit(solution)/shard_map/ppermute | solution.py:559
  9.8 5.1 %collective-permute-start.1 = (bf16[4,7,16,128]{3,2,1,0:T(8,128)(2,1)S(1)}, bf16[4,7,16,128]{3,2,1,0:T(8,128)(2,1)S(1)}, u32[]{:S(2)}, u32[]{:S(2)}) collective-permute-start(bf16[4,7,16,128]{3,2,1,0:T(8,128)(2,1)S(1)} %get-tuple-element.14), channel_id=1, source_target_pairs={{0,1},{1,0},{4,8},{5,9},{8,4},{9,5},{12,13},{13,12},{2,3},{3,2},{6... | collective-permute-start | bytes 344072 | tf_op jit(solution)/shard_map/ppermute | solution.py:559
  9.8 5.1 %copy-start = (bf16[2,48,144]{2,1,0:T(8,128)(2,1)S(1)}, bf16[2,48,144]{2,1,0:T(8,128)(2,1)}, u32[]{:S(2)}) copy-start(bf16[2,48,144]{2,1,0:T(8,128)(2,1)} %refs_9_.1) | copy-start | bytes 82948
  9.8 5.1 %copy-start.1 = (bf16[2,48,192]{2,1,0:T(8,128)(2,1)S(1)}, bf16[2,48,192]{2,1,0:T(8,128)(2,1)}, u32[]{:S(2)}) copy-start(bf16[2,48,192]{2,1,0:T(8,128)(2,1)} %refs_11_.1) | copy-start | bytes 110596
  9.8 5.1 %copy-start.2 = (bf16[2,192,48]{1,2,0:T(8,128)(2,1)S(1)}, bf16[2,192,48]{1,2,0:T(8,128)(2,1)}, u32[]{:S(2)}) copy-start(bf16[2,192,48]{1,2,0:T(8,128)(2,1)} %param.13) | copy-start | bytes 110596
  9.8 5.1 %copy-start.3 = (bf16[2,48,48]{2,1,0:T(8,128)(2,1)S(1)}, bf16[2,48,48]{2,1,0:T(8,128)(2,1)}, u32[]{:S(2)}) copy-start(bf16[2,48,48]{2,1,0:T(8,128)(2,1)} %refs_10_.3) | copy-start | bytes 27652
  9.8 5.1 %copy-start.4 = (f32[16,384]{1,0:T(8,128)S(1)}, f32[16,384]{1,0:T(8,128)}, u32[]{:S(2)}) copy-start(f32[16,384]{1,0:T(8,128)} %constant.35.clone.refs_1_.geo_ref) | copy-start | bytes 73732
  11.3 3.5 %copy-start.5 = (f32[2,2,48]{2,1,0:T(2,128)S(1)}, f32[2,2,48]{2,1,0:T(2,128)}, u32[]{:S(2)}) copy-start(f32[2,2,48]{2,1,0:T(2,128)} %refs_13_.1) | copy-start | bytes 2308
  11.3 6.7 %collective-permute-start.4 = (bf16[4,4,16,128]{3,2,1,0:T(8,128)(2,1)S(1)}, bf16[4,4,16,128]{3,2,1,0:T(8,128)(2,1)S(1)}, u32[]{:S(2)}, u32[]{:S(2)}) collective-permute-start(bf16[4,4,16,128]{3,2,1,0:T(8,128)(2,1)S(1)} %get-tuple-element.19), channel_id=1, source_target_pairs={{0,1},{1,0},{4,8},{5,9},{8,4},{9,5},{12,13},{13,12},{2,3},{3,2},{6... | collective-permute-start | bytes 196616 | tf_op jit(solution)/shard_map/ppermute | solution.py:559
  11.4 6.6 %collective-permute-start.3 = (bf16[4,4,16,128]{3,2,1,0:T(8,128)(2,1)S(1)}, bf16[4,4,16,128]{3,2,1,0:T(8,128)(2,1)S(1)}, u32[]{:S(2)}, u32[]{:S(2)}) collective-permute-start(bf16[4,4,16,128]{3,2,1,0:T(8,128)(2,1)S(1)} %get-tuple-element.20), channel_id=1, source_target_pairs={{0,4},{1,5},{4,0},{5,1},{8,12},{9,13},{12,8},{13,9},{2,6},{3,7},{6... | collective-permute-start | bytes 196616 | tf_op jit(solution)/shard_map/ppermute | solution.py:559
  17.9 3.4 %collective-permute-start.5 = (bf16[15,7,8,128]{3,2,1,0:T(8,128)(2,1)S(1)}, bf16[15,7,8,128]{3,2,1,0:T(8,128)(2,1)S(1)}, u32[]{:S(2)}, u32[]{:S(2)}) collective-permute-start(bf16[15,7,8,128]{3,2,1,0:T(8,128)(2,1)S(1)} %shard_map.93), channel_id=1, source_target_pairs={{0,1},{1,0},{2,3},{3,2},{4,5},{5,4},{6,7},{7,6},{8,9},{9,8},{10,11... | collective-permute-start | bytes 645128 | tf_op jit(solution)/shard_map/ppermute | solution.py:601
  18.1 3.3 %collective-permute-start.6 = (bf16[15,4,8,128]{3,2,1,0:T(8,128)(2,1)S(1)}, bf16[15,4,8,128]{3,2,1,0:T(8,128)(2,1)S(1)}, u32[]{:S(2)}, u32[]{:S(2)}) collective-permute-start(bf16[15,4,8,128]{3,2,1,0:T(8,128)(2,1)S(1)} %shard_map.94), channel_id=1, source_target_pairs={{0,1},{1,0},{2,3},{3,2},{4,5},{5,4},{6,7},{7,6},{8,9},{9,8},{10,11... | collective-permute-start | bytes 368648 | tf_op jit(solution)/shard_map/ppermute | solution.py:601

commit v3 on v2

--- a/solution.py
+++ b/solution.py
@@ -392,8 +392,9 @@
     early = ypieces == 1
     if early:
         free_ref, *refs = refs
-    pieces = refs[: 4 * (ypieces + 1)]
-    rest = refs[4 * (ypieces + 1) :]
+    pieces = refs[: 3 * (ypieces + 1)]
+    zs_ref = refs[3 * (ypieces + 1)]
+    rest = refs[3 * (ypieces + 1) + 1 :]
     wqkv_ref, wproj_ref, wup_ref, wdown_ref, gain_ref, wconv_hbm, cgain_hbm, out_ref = rest[:8]
     ext, mix, fed, grid, wc, tot, wconv_ref, cgain_ref, sems, ks, vs = rest[8:19]
     qs = rest[19:]
@@ -411,13 +412,13 @@
     xa, xb = [jnp.where(index[0] % 2 == k, far, 0) for k in (0, 1)]
     ys = [jnp.where(index[1] % 2 == k, far, 0) for k in range(2)]
     wts = block_weights(1, wqkv_ref, wproj_ref, wup_ref, wdown_ref, gain_ref)
-    tiles = []
+    tiles, at = [], 0
     for k, y in enumerate([HIGH] + ys[:ypieces]):
-        at = 0
         for i, x in enumerate((HIGH, xa, xb)):
-            mine = pieces[4 * k + i][:, :, -ROWS:, :]
-            tiles.append((mine, pieces[4 * k + 3][at : at + mine.shape[0]], x, y))
-            at += mine.shape[0]
+            mine = pieces[3 * k + i][:, :, -ROWS:, :]
+            n = mine.shape[0] * mine.shape[1]
+            tiles.append((mine, zs_ref[at : at + n], x, y))
+            at += n
     if ypieces == 1:
         ext[:, :, pl.ds(ys[1], HIGH)] = jnp.zeros((2, EXT, HIGH, ROWS, LANES), F32)
 
@@ -633,10 +634,11 @@
         def kernel(*refs):
             at = 0
             for r in refs[:-1]:
-                refs[-1][at : at + r.shape[0]] = r[:, :, -ROWS:, :]
-                at += r.shape[0]
-
-        shape = (sum(p.shape[0] for p in parts),) + (parts[0].shape[1], ROWS, LANES)
+                n = r.shape[0] * r.shape[1]
+                refs[-1][at : at + n] = r[:, :, -ROWS:, :].reshape(n, ROWS, LANES)
+                at += n
+
+        shape = (sum(p.shape[0] * p.shape[1] for p in parts), ROWS, LANES)
         return pl.pallas_call(
             kernel,
             out_shape=jax.ShapeDtypeStruct(shape, BF),
@@ -647,19 +649,16 @@
     wide = [v for y, c in zip(ys, corners) for v in (y, *c)]
     if len(ys) == 1:
         early = inner(-1, [geo, *near, *weights])
-        rows_first = lax.optimization_barrier((early, *near))
-        zs = other_core(edge(rows_first[1:]))
-        zcorners = [other_core(edge([y, *c])) for y, c in zip(ys, corners)]
+        waited = lax.optimization_barrier((early, *near))
+        zs = other_core(edge([*waited[1:], *wide]))
         done = inner(1, [geo, *near, *wide, *weights])
         done = [done, early]
     else:
-        zs = other_core(edge(near))
-        zcorners = [other_core(edge([y, *c])) for y, c in zip(ys, corners)]
+        zs = other_core(edge(near + wide))
         done = [inner(0, [geo, *near, *wide, *weights])]
 
-    flat = [v for y, c, z in zip(ys, corners, zcorners) for v in (y, *c, z)]
     conv = [pltpu.with_memory_space_constraint(v, pltpu.HBM) for v in (conv_weight, conv_gain[None, :])]
-    operands = [geo, *done, *near, zs, *flat, *weights, *conv]
+    operands = [geo, *done, *near, *wide, zs, *weights, *conv]
     vmem = pl.BlockSpec(memory_space=pltpu.VMEM)
     hbm = pl.BlockSpec(memory_space=pltpu.HBM)
     return pl.pallas_call(

time: 28.4 us -> 27.8 us (0.979)
  starting transfers between devices: 8.69 us -> 8.14 us
    ppermute x2 -> x1, starting transfers between devices: 0.61 us -> 0.07 us  [other_core(): return lax.ppermute(v, 'gz', [(0, 1), (1, 0)])]
  transfers between devices with their start and end apart: 7 -> 6, of which waited for: 1 -> 1; matrix products, arithmetic and copies ran while one was open for 0% -> 0% of each run, Pallas kernels for 21% -> 21%
where the time goes in v3:
time: 27.8 us; the launch traced here: 27.6 us
  Pallas kernels  17.6 us (63%)
  starting transfers between devices  8.14 us (29%)
  waiting for transfers between devices  1.54 us (6%)
  between operations  0.31 us (1%)
    ppermute x5, starting transfers between devices, exchange(): return lax.ppermute(v, (axis, 'gz'), pairs)  8.07 us
    pallas_call x1, Pallas kernels, body(): pl.pallas_call(functools.partial(last_kernel, width, len(ys)), out_shape=...  6.68 us
    pallas_call x2, Pallas kernels, inner(): pl.pallas_call(functools.partial(inner_kernel, width, len(ys), part), out...  5.73 us
    pallas_call x1, Pallas kernels, body(): pl.pallas_call(functools.partial(first_kernel, width, len(halves)), out_s...  5.14 us
    ppermute x5, waiting for transfers between devices, exchange(): return lax.ppermute(v, (axis, 'gz'), pairs)  1.54 us
  transfers between devices with their start and end apart: 6, of which 1 were waited for; matrix products, arithmetic and copies ran while one was open for 0% of the time, Pallas kernels for 21%

profile of v3, /device:TPU:0, one launch (start us, length us, event | category | flops | bytes accessed | tf_op | source)
XLA Modules:
  0.0 27.6 jit_solution(15514542619269879586)
XLA Ops:
  0.0 5.1 %first_block.1 = (bf16[7,7,16,128]{3,2,1,0:T(8,128)(2,1)S(1)}, bf16[7,4,16,128]{3,2,1,0:T(8,128)(2,1)S(1)}, bf16[4,7,16,128]{3,2,1,0:T(8,128)(2,1)S(1)}, bf16[4,7,16,128]{3,2,1,0:T(8,128)(2,1)S(1)}) custom-call(bf16[7,7,28,48]{3,2,1,0:T(8,128)(2,1)} %refs_0_.1, f32[16,384]{1,0:T(8,128)} %constant.35.clone.refs_1_.geo_ref, bf16[2,48,144]{2,1,0:T(8,128)(2,1)} %refs_8_.3, ...), custom_call_target="tpu_custom_call" | custom-call | tf_op jit(solution)/shard_map/first_block/pallas_call | solution.py:574
  5.2 3.0 %collective-permute-start.2 = (bf16[7,4,16,128]{3,2,1,0:T(8,128)(2,1)S(1)}, bf16[7,4,16,128]{3,2,1,0:T(8,128)(2,1)S(1)}, u32[]{:S(2)}, u32[]{:S(2)}) collective-permute-start(bf16[7,4,16,128]{3,2,1,0:T(8,128)(2,1)S(1)} %get-tuple-element.15), channel_id=1, source_target_pairs={{0,2},{1,3},{2,0},{3,1},{4,6},{5,7},{6,4},{7,5},{8,10},{9,11},{10,... | collective-permute-start | bytes 344072 | tf_op jit(solution)/shard_map/ppermute | solution.py:560
  8.2 1.6 %collective-permute-start = (bf16[4,7,16,128]{3,2,1,0:T(8,128)(2,1)S(1)}, bf16[4,7,16,128]{3,2,1,0:T(8,128)(2,1)S(1)}, u32[]{:S(2)}, u32[]{:S(2)}) collective-permute-start(bf16[4,7,16,128]{3,2,1,0:T(8,128)(2,1)S(1)} %get-tuple-element.13), channel_id=1, source_target_pairs={{0,4},{1,5},{4,0},{5,1},{8,12},{9,13},{12,8},{13,9},{2,6},{3,7},{6... | collective-permute-start | bytes 344072 | tf_op jit(solution)/shard_map/ppermute | solution.py:560
  9.8 0.0 collective-permute-start.1
  9.8 0.0 copy-start.3
  9.8 0.0 copy-start.4
  9.8 1.5 %collective-permute-done.2.refs_3_.refs_4_ = bf16[7,4,16,128]{3,2,1,0:T(8,128)(2,1)S(1)} collective-permute-done((bf16[7,4,16,128]{3,2,1,0:T(8,128)(2,1)S(1)}, bf16[7,4,16,128]{3,2,1,0:T(8,128)(2,1)S(1)}, u32[]{:S(2)}, u32[]{:S(2)}) %collective-permute-start.2) | collective-permute-done | bytes 114720 | tf_op jit(solution)/shard_map/ppermute | solution.py:560
  11.3 0.0 copy-start.5
  11.3 0.1 collective-permute-start.4
  11.4 3.4 %collective-permute-start.3 = (bf16[4,4,16,128]{3,2,1,0:T(8,128)(2,1)S(1)}, bf16[4,4,16,128]{3,2,1,0:T(8,128)(2,1)S(1)}, u32[]{:S(2)}, u32[]{:S(2)}) collective-permute-start(bf16[4,4,16,128]{3,2,1,0:T(8,128)(2,1)S(1)} %get-tuple-element.20), channel_id=1, source_target_pairs={{0,4},{1,5},{4,0},{5,1},{8,12},{9,13},{12,8},{13,9},{2,6},{3,7},{6... | collective-permute-start | bytes 196616 | tf_op jit(solution)/shard_map/ppermute | solution.py:560
  14.8 0.0 collective-permute-done.refs_1_.refs_2_
  14.8 0.0 collective-permute-done.1.refs_2_.refs_3_
  14.8 0.0 copy-done
  14.8 0.0 copy-done.1
  14.8 0.0 copy-done.2
  14.9 0.0 copy-done.3
  14.9 3.0 %shard_map.92.refs_0_ = f32[1152,128]{1,0:T(8,128)S(1)} custom-call(f32[16,384]{1,0:T(8,128)S(1)} %copy-done.4, bf16[7,7,16,128]{3,2,1,0:T(8,128)(2,1)S(1)} %get-tuple-element.16.refs_0_.refs_1_, bf16[4,7,16,128]{3,2,1,0:T(8,128)(2,1)S(1)} %collective-permute-done.refs_1_.refs_2_, bf16[4,7,16,128]{3,2,1,0:T(8,128)(2,1)S(1)} %collective-permute-done.1.refs_2_.refs_3_, ...), custom_call_target="tpu_custom_call" | custom-call | flops 2000000000 | bytes 1000000 | tf_op jit(solution)/shard_map/pallas_call | solution.py:621
  17.9 0.0 collective-permute-done.4.refs_5_.refs_6_
  17.9 0.0 collective-permute-done.3.refs_4_.refs_5_
  17.9 0.1 shard_map.93
  18.0 0.1 collective-permute-start.5
  18.0 2.7 %shard_map.91.inner_ref = f32[1152,128]{1,0:T(8,128)S(1)} custom-call(f32[16,384]{1,0:T(8,128)S(1)} %copy-done.4, bf16[7,7,16,128]{3,2,1,0:T(8,128)(2,1)S(1)} %get-tuple-element.16.refs_0_.refs_1_, bf16[4,7,16,128]{3,2,1,0:T(8,128)(2,1)S(1)} %collective-permute-done.refs_1_.refs_2_, bf16[4,7,16,128]{3,2,1,0:T(8,128)(2,1)S(1)} %collective-permute-done.1.refs_2_.refs_3_, ...), custom_call_target="tpu_custom_call" | custom-call | flops 2000000000 | bytes 1000000 | tf_op jit(solution)/shard_map/pallas_call | solution.py:621
  20.8 0.0 collective-permute-done.5.refs_7_
  20.8 6.7 %last_windows.1 = bf16[7,7,28,48]{3,2,1,0:T(8,128)(2,1)} custom-call(f32[16,384]{1,0:T(8,128)S(1)} %copy-done.4, f32[1152,128]{1,0:T(8,128)S(1)} %shard_map.91.inner_ref, f32[1152,128]{1,0:T(8,128)S(1)} %shard_map.92.refs_0_, bf16[7,7,16,128]{3,2,1,0:T(8,128)(2,1)S(1)} %get-tuple-element.16.refs_0_.refs_1_, ...), custom_call_target="tpu_custom_call" | custom-call | tf_op jit(solution)/shard_map/last_windows/pallas_call | solution.py:664
  (6 shorter events, 0.0 us)
Async XLA Ops:
  5.2 6.2 %collective-permute-start.2 = (bf16[7,4,16,128]{3,2,1,0:T(8,128)(2,1)S(1)}, bf16[7,4,16,128]{3,2,1,0:T(8,128)(2,1)S(1)}, u32[]{:S(2)}, u32[]{:S(2)}) collective-permute-start(bf16[7,4,16,128]{3,2,1,0:T(8,128)(2,1)S(1)} %get-tuple-element.15), channel_id=1, source_target_pairs={{0,2},{1,3},{2,0},{3,1},{4,6},{5,7},{6,4},{7,5},{8,10},{9,11},{10,... | collective-permute-start | bytes 344072 | tf_op jit(solution)/shard_map/ppermute | solution.py:560
  8.2 6.6 %collective-permute-start = (bf16[4,7,16,128]{3,2,1,0:T(8,128)(2,1)S(1)}, bf16[4,7,16,128]{3,2,1,0:T(8,128)(2,1)S(1)}, u32[]{:S(2)}, u32[]{:S(2)}) collective-permute-start(bf16[4,7,16,128]{3,2,1,0:T(8,128)(2,1)S(1)} %get-tuple-element.13), channel_id=1, source_target_pairs={{0,4},{1,5},{4,0},{5,1},{8,12},{9,13},{12,8},{13,9},{2,6},{3,7},{6... | collective-permute-start | bytes 344072 | tf_op jit(solution)/shard_map/ppermute | solution.py:560
  9.8 5.1 %collective-permute-start.1 = (bf16[4,7,16,128]{3,2,1,0:T(8,128)(2,1)S(1)}, bf16[4,7,16,128]{3,2,1,0:T(8,128)(2,1)S(1)}, u32[]{:S(2)}, u32[]{:S(2)}) collective-permute-start(bf16[4,7,16,128]{3,2,1,0:T(8,128)(2,1)S(1)} %get-tuple-element.14), channel_id=1, source_target_pairs={{0,1},{1,0},{4,8},{5,9},{8,4},{9,5},{12,13},{13,12},{2,3},{3,2},{6... | collective-permute-start | bytes 344072 | tf_op jit(solution)/shard_map/ppermute | solution.py:560
  9.8 5.1 %copy-start = (bf16[2,48,144]{2,1,0:T(8,128)(2,1)S(1)}, bf16[2,48,144]{2,1,0:T(8,128)(2,1)}, u32[]{:S(2)}) copy-start(bf16[2,48,144]{2,1,0:T(8,128)(2,1)} %refs_8_.3) | copy-start | bytes 82948
  9.8 5.1 %copy-start.1 = (bf16[2,48,192]{2,1,0:T(8,128)(2,1)S(1)}, bf16[2,48,192]{2,1,0:T(8,128)(2,1)}, u32[]{:S(2)}) copy-start(bf16[2,48,192]{2,1,0:T(8,128)(2,1)} %refs_10_.3) | copy-start | bytes 110596
  9.8 5.1 %copy-start.2 = (bf16[2,192,48]{1,2,0:T(8,128)(2,1)S(1)}, bf16[2,192,48]{1,2,0:T(8,128)(2,1)}, u32[]{:S(2)}) copy-start(bf16[2,192,48]{1,2,0:T(8,128)(2,1)} %param.13) | copy-start | bytes 110596
  9.8 5.1 %copy-start.3 = (bf16[2,48,48]{2,1,0:T(8,128)(2,1)S(1)}, bf16[2,48,48]{2,1,0:T(8,128)(2,1)}, u32[]{:S(2)}) copy-start(bf16[2,48,48]{2,1,0:T(8,128)(2,1)} %refs_9_.1) | copy-start | bytes 27652
  9.8 5.1 %copy-start.4 = (f32[16,384]{1,0:T(8,128)S(1)}, f32[16,384]{1,0:T(8,128)}, u32[]{:S(2)}) copy-start(f32[16,384]{1,0:T(8,128)} %constant.35.clone.refs_1_.geo_ref) | copy-start | bytes 73732
  11.3 3.5 %copy-start.5 = (f32[2,2,48]{2,1,0:T(2,128)S(1)}, f32[2,2,48]{2,1,0:T(2,128)}, u32[]{:S(2)}) copy-start(f32[2,2,48]{2,1,0:T(2,128)} %refs_12_.1) | copy-start | bytes 2308
  11.3 6.5 %collective-permute-start.4 = (bf16[4,4,16,128]{3,2,1,0:T(8,128)(2,1)S(1)}, bf16[4,4,16,128]{3,2,1,0:T(8,128)(2,1)S(1)}, u32[]{:S(2)}, u32[]{:S(2)}) collective-permute-start(bf16[4,4,16,128]{3,2,1,0:T(8,128)(2,1)S(1)} %get-tuple-element.19), channel_id=1, source_target_pairs={{0,1},{1,0},{4,8},{5,9},{8,4},{9,5},{12,13},{13,12},{2,3},{3,2},{6... | collective-permute-start | bytes 196616 | tf_op jit(solution)/shard_map/ppermute | solution.py:560
  11.4 6.5 %collective-permute-start.3 = (bf16[4,4,16,128]{3,2,1,0:T(8,128)(2,1)S(1)}, bf16[4,4,16,128]{3,2,1,0:T(8,128)(2,1)S(1)}, u32[]{:S(2)}, u32[]{:S(2)}) collective-permute-start(bf16[4,4,16,128]{3,2,1,0:T(8,128)(2,1)S(1)} %get-tuple-element.20), channel_id=1, source_target_pairs={{0,4},{1,5},{4,0},{5,1},{8,12},{9,13},{12,8},{13,9},{2,6},{3,7},{6... | collective-permute-start | bytes 196616 | tf_op jit(solution)/shard_map/ppermute | solution.py:560
  18.0 2.8 %collective-permute-start.5 = (bf16[165,8,128]{2,1,0:T(8,128)(2,1)S(1)}, bf16[165,8,128]{2,1,0:T(8,128)(2,1)S(1)}, u32[]{:S(2)}, u32[]{:S(2)}) collective-permute-start(bf16[165,8,128]{2,1,0:T(8,128)(2,1)S(1)} %shard_map.93), channel_id=1, source_target_pairs={{0,1},{1,0},{2,3},{3,2},{4,5},{5,4},{6,7},{7,6},{8,9},{9,8},{10,11... | collective-permute-start | bytes 1013768 | tf_op jit(solution)/shard_map/ppermute | solution.py:602

commit v4 on v3

--- a/solution.py
+++ b/solution.py
@@ -164,17 +164,17 @@
         mixed = mix[w0 : w0 + n].reshape(n * keys, LANES)[:, :width].astype(BF)
         first = held[:, keys * w0 : keys * (w0 + n)] + against_rows(wts[3][:, :width], mixed)
         out = feed(first, wts, width)
-        out = jnp.transpose(jnp.concatenate([out, jnp.zeros((LANES - width, n * keys), F32)], 0))[:, :width]
-        out = out.reshape(n, kept, ROWS, width)
+        nil = jnp.zeros((HALF - width, n * keys), F32)
+        out = jnp.transpose(jnp.concatenate([out, nil, out, nil], 0)).reshape(n, kept, ROWS, LANES)
         for w in range(w0, w0 + n):
-            done[0:kept, WINDOW * w : WINDOW * (w + 1), :width] = out[w - w0, :, :WINDOW, :]
+            done[0:kept, WINDOW * w : WINDOW * (w + 1), :] = out[w - w0, :, :WINDOW, :]
             if w == 0:
-                done[0:kept, nz : nz + SHIFT, :width] = out[w - w0, :, :SHIFT, :]
+                done[0:kept, nz : nz + SHIFT, :] = out[w - w0, :, :SHIFT, :]
             for j in range(WINDOW):
                 one = out[w - w0, j, WINDOW : WINDOW + 1, :]
-                done[kept, WINDOW * w + j : WINDOW * w + j + 1, :width] = one
+                done[kept, WINDOW * w + j : WINDOW * w + j + 1, :] = one
                 if w == 0 and j < SHIFT:
-                    done[kept, nz + j : nz + j + 1, :width] = one
+                    done[kept, nz + j : nz + j + 1, :] = one
 
     for w in range(groups):
         make(w)
@@ -188,8 +188,8 @@
     attend([(qs.at[w], ks.at[w], vs.at[w], keys, keep(w)) for w in range(groups)], width)
     finish(0, groups)
     pieces = [done[:, SHIFT + WINDOW * w : SHIFT + WINDOW * w + ROWS, :] for w in range(groups)]
-    rolled = [pltpu.roll(p.reshape(spots * ROWS, LANES), HALF, 1).reshape(spots, ROWS, LANES) for p in pieces[1::2]]
-    joined = [a + b for a, b in zip(pieces[0::2], rolled)]
+    lower = iota(pieces[0].shape, 2) < HALF
+    joined = [jnp.where(lower, a, b) for a, b in zip(pieces[0::2], pieces[1::2])]
     packed = jnp.concatenate(joined, 1).astype(BF)
     out_ref[...] = packed.reshape(WINDOW, WINDOW, ROWS * len(joined), LANES)
     yodd = lax.axis_index("gy") % 2

time: 27.8 us -> 27.7 us (level)
  no operation moved by 1% of the time
where the time goes in v4:
time: 27.7 us; the launch traced here: 27.5 us
  Pallas kernels  17.5 us (63%)
  starting transfers between devices  8.14 us (29%)
  waiting for transfers between devices  1.54 us (6%)
  between operations  0.31 us (1%)
    ppermute x5, starting transfers between devices, exchange(): return lax.ppermute(v, (axis, 'gz'), pairs)  8.07 us
    pallas_call x1, Pallas kernels, body(): pl.pallas_call(functools.partial(last_kernel, width, len(ys)), out_shape=...  6.68 us
    pallas_call x2, Pallas kernels, inner(): pl.pallas_call(functools.partial(inner_kernel, width, len(ys), part), out...  5.72 us
    pallas_call x1, Pallas kernels, body(): pl.pallas_call(functools.partial(first_kernel, width, len(halves)), out_s...  5.02 us
    ppermute x5, waiting for transfers between devices, exchange(): return lax.ppermute(v, (axis, 'gz'), pairs)  1.54 us
  transfers between devices with their start and end apart: 6, of which 1 were waited for; matrix products, arithmetic and copies ran while one was open for 0% of the time, Pallas kernels for 21%

profile of v4, /device:TPU:0, one launch (start us, length us, event | category | flops | bytes accessed | tf_op | source)
XLA Modules:
  0.0 27.5 jit_solution(7657906640871080222)
XLA Ops:
  0.0 5.0 %first_block.1 = (bf16[7,7,16,128]{3,2,1,0:T(8,128)(2,1)S(1)}, bf16[7,4,16,128]{3,2,1,0:T(8,128)(2,1)S(1)}, bf16[4,7,16,128]{3,2,1,0:T(8,128)(2,1)S(1)}, bf16[4,7,16,128]{3,2,1,0:T(8,128)(2,1)S(1)}) custom-call(bf16[7,7,28,48]{3,2,1,0:T(8,128)(2,1)} %refs_0_.1, f32[16,384]{1,0:T(8,128)} %constant.35.clone.refs_1_.geo_ref, bf16[2,48,144]{2,1,0:T(8,128)(2,1)} %refs_8_.3, ...), custom_call_target="tpu_custom_call" | custom-call | tf_op jit(solution)/shard_map/first_block/pallas_call | solution.py:574
  5.0 3.0 %collective-permute-start.2 = (bf16[7,4,16,128]{3,2,1,0:T(8,128)(2,1)S(1)}, bf16[7,4,16,128]{3,2,1,0:T(8,128)(2,1)S(1)}, u32[]{:S(2)}, u32[]{:S(2)}) collective-permute-start(bf16[7,4,16,128]{3,2,1,0:T(8,128)(2,1)S(1)} %get-tuple-element.15), channel_id=1, source_target_pairs={{0,2},{1,3},{2,0},{3,1},{4,6},{5,7},{6,4},{7,5},{8,10},{9,11},{10,... | collective-permute-start | bytes 344072 | tf_op jit(solution)/shard_map/ppermute | solution.py:560
  8.1 1.6 %collective-permute-start = (bf16[4,7,16,128]{3,2,1,0:T(8,128)(2,1)S(1)}, bf16[4,7,16,128]{3,2,1,0:T(8,128)(2,1)S(1)}, u32[]{:S(2)}, u32[]{:S(2)}) collective-permute-start(bf16[4,7,16,128]{3,2,1,0:T(8,128)(2,1)S(1)} %get-tuple-element.13), channel_id=1, source_target_pairs={{0,4},{1,5},{4,0},{5,1},{8,12},{9,13},{12,8},{13,9},{2,6},{3,7},{6... | collective-permute-start | bytes 344072 | tf_op jit(solution)/shard_map/ppermute | solution.py:560
  9.6 0.0 collective-permute-start.1
  9.6 0.0 copy-start.3
  9.7 0.0 copy-start.4
  9.7 1.5 %collective-permute-done.2.refs_3_.refs_4_ = bf16[7,4,16,128]{3,2,1,0:T(8,128)(2,1)S(1)} collective-permute-done((bf16[7,4,16,128]{3,2,1,0:T(8,128)(2,1)S(1)}, bf16[7,4,16,128]{3,2,1,0:T(8,128)(2,1)S(1)}, u32[]{:S(2)}, u32[]{:S(2)}) %collective-permute-start.2) | collective-permute-done | bytes 114720 | tf_op jit(solution)/shard_map/ppermute | solution.py:560
  11.2 0.0 copy-start.5
  11.2 0.1 collective-permute-start.4
  11.3 3.4 %collective-permute-start.3 = (bf16[4,4,16,128]{3,2,1,0:T(8,128)(2,1)S(1)}, bf16[4,4,16,128]{3,2,1,0:T(8,128)(2,1)S(1)}, u32[]{:S(2)}, u32[]{:S(2)}) collective-permute-start(bf16[4,4,16,128]{3,2,1,0:T(8,128)(2,1)S(1)} %get-tuple-element.20), channel_id=1, source_target_pairs={{0,4},{1,5},{4,0},{5,1},{8,12},{9,13},{12,8},{13,9},{2,6},{3,7},{6... | collective-permute-start | bytes 196616 | tf_op jit(solution)/shard_map/ppermute | solution.py:560
  14.7 0.0 collective-permute-done.refs_1_.refs_2_
  14.7 0.0 collective-permute-done.1.refs_2_.refs_3_
  14.7 0.0 copy-done
  14.7 0.0 copy-done.1
  14.7 0.0 copy-done.2
  14.7 0.0 copy-done.3
  14.8 3.0 %shard_map.92.refs_0_ = f32[1152,128]{1,0:T(8,128)S(1)} custom-call(f32[16,384]{1,0:T(8,128)S(1)} %copy-done.4, bf16[7,7,16,128]{3,2,1,0:T(8,128)(2,1)S(1)} %get-tuple-element.16.refs_0_.refs_1_, bf16[4,7,16,128]{3,2,1,0:T(8,128)(2,1)S(1)} %collective-permute-done.refs_1_.refs_2_, bf16[4,7,16,128]{3,2,1,0:T(8,128)(2,1)S(1)} %collective-permute-done.1.refs_2_.refs_3_, ...), custom_call_target="tpu_custom_call" | custom-call | flops 2000000000 | bytes 1000000 | tf_op jit(solution)/shard_map/pallas_call | solution.py:621
  17.8 0.0 collective-permute-done.4.refs_5_.refs_6_
  17.8 0.0 collective-permute-done.3.refs_4_.refs_5_
  17.8 0.1 shard_map.93
  17.8 0.1 collective-permute-start.5
  17.9 2.7 %shard_map.91.inner_ref = f32[1152,128]{1,0:T(8,128)S(1)} custom-call(f32[16,384]{1,0:T(8,128)S(1)} %copy-done.4, bf16[7,7,16,128]{3,2,1,0:T(8,128)(2,1)S(1)} %get-tuple-element.16.refs_0_.refs_1_, bf16[4,7,16,128]{3,2,1,0:T(8,128)(2,1)S(1)} %collective-permute-done.refs_1_.refs_2_, bf16[4,7,16,128]{3,2,1,0:T(8,128)(2,1)S(1)} %collective-permute-done.1.refs_2_.refs_3_, ...), custom_call_target="tpu_custom_call" | custom-call | flops 2000000000 | bytes 1000000 | tf_op jit(solution)/shard_map/pallas_call | solution.py:621
  20.7 0.0 collective-permute-done.5.refs_7_
  20.7 6.7 %last_windows.1 = bf16[7,7,28,48]{3,2,1,0:T(8,128)(2,1)} custom-call(f32[16,384]{1,0:T(8,128)S(1)} %copy-done.4, f32[1152,128]{1,0:T(8,128)S(1)} %shard_map.91.inner_ref, f32[1152,128]{1,0:T(8,128)S(1)} %shard_map.92.refs_0_, bf16[7,7,16,128]{3,2,1,0:T(8,128)(2,1)S(1)} %get-tuple-element.16.refs_0_.refs_1_, ...), custom_call_target="tpu_custom_call" | custom-call | tf_op jit(solution)/shard_map/last_windows/pallas_call | solution.py:664
  (6 shorter events, 0.0 us)
Async XLA Ops:
  5.0 6.2 %collective-permute-start.2 = (bf16[7,4,16,128]{3,2,1,0:T(8,128)(2,1)S(1)}, bf16[7,4,16,128]{3,2,1,0:T(8,128)(2,1)S(1)}, u32[]{:S(2)}, u32[]{:S(2)}) collective-permute-start(bf16[7,4,16,128]{3,2,1,0:T(8,128)(2,1)S(1)} %get-tuple-element.15), channel_id=1, source_target_pairs={{0,2},{1,3},{2,0},{3,1},{4,6},{5,7},{6,4},{7,5},{8,10},{9,11},{10,... | collective-permute-start | bytes 344072 | tf_op jit(solution)/shard_map/ppermute | solution.py:560
  8.1 6.6 %collective-permute-start = (bf16[4,7,16,128]{3,2,1,0:T(8,128)(2,1)S(1)}, bf16[4,7,16,128]{3,2,1,0:T(8,128)(2,1)S(1)}, u32[]{:S(2)}, u32[]{:S(2)}) collective-permute-start(bf16[4,7,16,128]{3,2,1,0:T(8,128)(2,1)S(1)} %get-tuple-element.13), channel_id=1, source_target_pairs={{0,4},{1,5},{4,0},{5,1},{8,12},{9,13},{12,8},{13,9},{2,6},{3,7},{6... | collective-permute-start | bytes 344072 | tf_op jit(solution)/shard_map/ppermute | solution.py:560
  9.6 5.1 %collective-permute-start.1 = (bf16[4,7,16,128]{3,2,1,0:T(8,128)(2,1)S(1)}, bf16[4,7,16,128]{3,2,1,0:T(8,128)(2,1)S(1)}, u32[]{:S(2)}, u32[]{:S(2)}) collective-permute-start(bf16[4,7,16,128]{3,2,1,0:T(8,128)(2,1)S(1)} %get-tuple-element.14), channel_id=1, source_target_pairs={{0,1},{1,0},{4,8},{5,9},{8,4},{9,5},{12,13},{13,12},{2,3},{3,2},{6... | collective-permute-start | bytes 344072 | tf_op jit(solution)/shard_map/ppermute | solution.py:560
  9.6 5.1 %copy-start = (bf16[2,48,144]{2,1,0:T(8,128)(2,1)S(1)}, bf16[2,48,144]{2,1,0:T(8,128)(2,1)}, u32[]{:S(2)}) copy-start(bf16[2,48,144]{2,1,0:T(8,128)(2,1)} %refs_8_.3) | copy-start | bytes 82948
  9.6 5.1 %copy-start.1 = (bf16[2,48,192]{2,1,0:T(8,128)(2,1)S(1)}, bf16[2,48,192]{2,1,0:T(8,128)(2,1)}, u32[]{:S(2)}) copy-start(bf16[2,48,192]{2,1,0:T(8,128)(2,1)} %refs_10_.3) | copy-start | bytes 110596
  9.6 5.1 %copy-start.2 = (bf16[2,192,48]{1,2,0:T(8,128)(2,1)S(1)}, bf16[2,192,48]{1,2,0:T(8,128)(2,1)}, u32[]{:S(2)}) copy-start(bf16[2,192,48]{1,2,0:T(8,128)(2,1)} %param.13) | copy-start | bytes 110596
  9.6 5.1 %copy-start.3 = (bf16[2,48,48]{2,1,0:T(8,128)(2,1)S(1)}, bf16[2,48,48]{2,1,0:T(8,128)(2,1)}, u32[]{:S(2)}) copy-start(bf16[2,48,48]{2,1,0:T(8,128)(2,1)} %refs_9_.1) | copy-start | bytes 27652
  9.7 5.1 %copy-start.4 = (f32[16,384]{1,0:T(8,128)S(1)}, f32[16,384]{1,0:T(8,128)}, u32[]{:S(2)}) copy-start(f32[16,384]{1,0:T(8,128)} %constant.35.clone.refs_1_.geo_ref) | copy-start | bytes 73732
  11.2 3.5 %copy-start.5 = (f32[2,2,48]{2,1,0:T(2,128)S(1)}, f32[2,2,48]{2,1,0:T(2,128)}, u32[]{:S(2)}) copy-start(f32[2,2,48]{2,1,0:T(2,128)} %refs_12_.1) | copy-start | bytes 2308
  11.2 6.5 %collective-permute-start.4 = (bf16[4,4,16,128]{3,2,1,0:T(8,128)(2,1)S(1)}, bf16[4,4,16,128]{3,2,1,0:T(8,128)(2,1)S(1)}, u32[]{:S(2)}, u32[]{:S(2)}) collective-permute-start(bf16[4,4,16,128]{3,2,1,0:T(8,128)(2,1)S(1)} %get-tuple-element.19), channel_id=1, source_target_pairs={{0,1},{1,0},{4,8},{5,9},{8,4},{9,5},{12,13},{13,12},{2,3},{3,2},{6... | collective-permute-start | bytes 196616 | tf_op jit(solution)/shard_map/ppermute | solution.py:560
  11.3 6.5 %collective-permute-start.3 = (bf16[4,4,16,128]{3,2,1,0:T(8,128)(2,1)S(1)}, bf16[4,4,16,128]{3,2,1,0:T(8,128)(2,1)S(1)}, u32[]{:S(2)}, u32[]{:S(2)}) collective-permute-start(bf16[4,4,16,128]{3,2,1,0:T(8,128)(2,1)S(1)} %get-tuple-element.20), channel_id=1, source_target_pairs={{0,4},{1,5},{4,0},{5,1},{8,12},{9,13},{12,8},{13,9},{2,6},{3,7},{6... | collective-permute-start | bytes 196616 | tf_op jit(solution)/shard_map/ppermute | solution.py:560
  17.8 2.8 %collective-permute-start.5 = (bf16[165,8,128]{2,1,0:T(8,128)(2,1)S(1)}, bf16[165,8,128]{2,1,0:T(8,128)(2,1)S(1)}, u32[]{:S(2)}, u32[]{:S(2)}) collective-permute-start(bf16[165,8,128]{2,1,0:T(8,128)(2,1)S(1)} %shard_map.93), channel_id=1, source_target_pairs={{0,1},{1,0},{2,3},{3,2},{4,5},{5,4},{6,7},{7,6},{8,9},{9,8},{10,11... | collective-permute-start | bytes 1013768 | tf_op jit(solution)/shard_map/ppermute | solution.py:602
